TPU v7x, 32 devices: a whole 2x2x4 slice. The times are simulated.
32 devices in a mesh: section: 4 (over y, x), owner: 8 (over z, core).
Axes of the slice: x: 2, y: 2, z: 4, core: 2. Of those that a mesh axis runs over, the one named last changes fastest.
Arguments:
- probe_values: bfloat16 [8, 8192, 128], P('section', 'owner'), may hold values from -6 to 6
- probe_keys: int32 [8, 8192], P('section', 'owner'), may hold values from 0 to 2047
- group_ids: int32 [8, 8192], P('section', 'owner'), may hold values from 0 to 127
- block_dest: int32 [8, 64, 1], P('section', 'owner'), may hold values from 0 to 7; in each aligned block of 8 rows (0 to 7, 8 to 15, ..., all dimensions but the last counted through in order) at most 2 rows name the same one
- filter_bits: int32 [4, 8, 512], P('section', None, 'owner'), may hold values from 0 to 65535, as said below
- section_weights: bfloat16 [4, 128, 128], P('section'), may hold values from -0.5 to 0.5
- build_keys: int32 [32768], P('owner'), may hold values from 0 to 2047
- build_values: bfloat16 [32768, 128], P('owner'), may hold values from -6 to 6
Outputs:
- group_sums: float32 [128, 128], P(('section', 'owner'))
Inputs may be any that keep to these rules, and one draw needn't show every extreme that they name: `block_dest`: in each micro-batch, no owner is named by more than 2 of the 8 blocks of one device, a bound that some block reaches. `filter_bits`: bit b of a word is the keep bit of row 16 w + b; the upper bits are 0.
All inputs are finite; a program needn't handle non-finite values.
Results may differ from a plain program's by a relative error of at most 0.012.
Values may be sent and summed in bfloat16 or wider, within the bound.
No kernel may reach another device: no remote copies, remote signals or barrier semaphores. Data moves between devices by JAX's collectives and lax.ppermute only.
A program may use at most 128 MiB of HBM per device.

v0:
```python
import functools
import math

import jax
import jax.numpy as jnp
from jax import lax
from jax.experimental import pallas as pl
from jax.experimental.pallas import tpu as pltpu
from jax.sharding import PartitionSpec as P


CAP = 2
KEYS_OWN = 2048
GRP_DEV = 4
FIELDS = 4
BF16 = jnp.bfloat16
F32 = jnp.float32
I32 = jnp.int32


def run(kernel, ins, outs, scratch=(), scalars=(), flops=0, away=False):
    several = isinstance(outs, list)
    shapes = [jax.ShapeDtypeStruct(shape, dtype) for shape, dtype in (outs if several else [outs])]
    held = shapes + [x for k, x in enumerate(ins) if k not in scalars and not away]
    size = sum(math.prod(x.shape) * x.dtype.itemsize for x in held)
    for entry in scratch:
        size += 2 * math.prod(getattr(entry, "shape", ())) * 4
    place = pl.BlockSpec(memory_space=pltpu.VMEM)
    spaces = [pltpu.HBM if away else pltpu.SMEM if k in scalars else pltpu.VMEM for k in range(len(ins))]
    return pl.pallas_call(
        kernel,
        out_shape=shapes if several else shapes[0],
        in_specs=[pl.BlockSpec(memory_space=space) for space in spaces],
        out_specs=[place] * len(shapes) if several else place,
        scratch_shapes=list(scratch),
        compiler_params=pltpu.CompilerParams(vmem_limit_bytes=60 * 2**20 if away else min(size + 4 * 2**20, 60 * 2**20)),
        cost_estimate=pl.CostEstimate(flops=flops, bytes_accessed=size, transcendentals=0) if flops else None,
    )(*ins)


def walk_blocks(dest_ref, count_ref, owners, visit):
    batches, blocks = dest_ref.shape

    def clear(owner, carry):
        count_ref[owner] = 0
        return carry

    lax.fori_loop(0, owners, clear, 0)
    for micro in range(batches):

        def step(block, carry, micro=micro):
            owner = dest_ref[micro, block]
            slot = count_ref[owner]
            count_ref[owner] = slot + 1
            visit(micro, block, owner, slot)
            return carry

        lax.fori_loop(0, blocks, step, 0, unroll=min(blocks, 8))


def put_block(slots, field_base, source, owner_at, slot, out_ref, meta_ref):
    values, keys, groups = source
    rows = values.shape[0]
    out_ref[owner_at, pl.ds(pl.multiple_of(slot * rows, rows), rows), :] = values
    for field, part in enumerate((keys >> 7, keys & 127, groups >> 7, groups & 127)):
        meta_ref[owner_at, pl.ds(field_base + field * slots + slot, 1), :] = part.astype(F32)


def pack_first(early, *refs):
    sources, (out_ref, dest_ref, values_ref, keys_ref, groups_ref, meta_ref, count_ref, sems) = refs[:4], refs[4:]
    owners = out_ref.shape[0]
    blocks = dest_ref.shape[1]
    rows = values_ref.shape[1]
    copies = [
        pltpu.make_async_copy(source, target, sems.at[k])
        for k, (source, target) in enumerate(zip(sources, (dest_ref, values_ref, keys_ref, groups_ref)))
    ]
    for copy in copies:
        copy.start()
    meta_ref[...] = jnp.zeros_like(meta_ref)
    out_ref[...] = jnp.zeros_like(out_ref)
    for copy in copies:
        copy.wait()

    def visit(micro, block, owner, slot):
        @pl.when(slot < early)
        def _():
            lanes = pl.ds(pl.multiple_of(block * rows, rows), rows)
            source = (values_ref[micro * blocks + block], keys_ref[pl.ds(micro, 1), lanes], groups_ref[pl.ds(micro, 1), lanes])
            put_block(early, 0, source, owner, slot, out_ref, meta_ref)

    walk_blocks(dest_ref, count_ref, owners, visit)
    out_ref[:, early * rows :, :] = meta_ref[...].astype(BF16)


def build_table(keys_ref, values_ref, out_ref, wide_ref):
    chunks, lanes = keys_ref.shape
    columns = values_ref.shape[1]
    tiles = out_ref.shape[0] // lanes // 2
    sub = lax.broadcasted_iota(I32, (lanes, lanes), 0)
    keys = keys_ref[...]
    upper = jnp.where(keys >= tiles * lanes, 1.0, 0.0).T
    middle = (keys >> 7) & (tiles - 1)
    low = []
    for chunk in range(chunks):
        low.append(jnp.where(sub == (keys[chunk : chunk + 1] & (lanes - 1)), 1.0, 0.0).astype(BF16))
        flag = jnp.broadcast_to(upper[:, chunk : chunk + 1], (lanes, columns)).astype(BF16)
        part = values_ref[chunk * lanes : (chunk + 1) * lanes, :]
        high_part = part * flag
        wide_ref[chunk * lanes : (chunk + 1) * lanes, :columns] = part - high_part
        wide_ref[chunk * lanes : (chunk + 1) * lanes, columns:] = high_part

    def tile_step(tile, carry):
        here = jnp.where(middle == tile, 1.0, 0.0)
        hot = [low[chunk] * jnp.broadcast_to(here[chunk : chunk + 1], (lanes, lanes)).astype(BF16) for chunk in range(chunks)]
        total = jnp.dot(jnp.concatenate(hot, axis=1), wide_ref[...], preferred_element_type=F32)
        out_ref[pl.ds(pl.multiple_of(tile * lanes, lanes), lanes), :] = total[:, :columns]
        out_ref[pl.ds(pl.multiple_of((tiles + tile) * lanes, lanes), lanes), :] = total[:, columns:]
        return carry

    lax.fori_loop(0, tiles, tile_step, 0)


def pack_last(sections, paired, early, late, scalar_ref, *refs):
    shared, (values_ref, keys_ref, groups_ref, dest_ref), refs = refs[:sections], refs[sections : sections + 4], refs[sections + 4 :]
    weights_ref, outs, (buffer_ref, meta_ref, kept_ref, count_ref) = refs[0], refs[1:-4], refs[-4:]
    owners = buffer_ref.shape[0]
    batches, blocks = dest_ref.shape
    rows = values_ref.shape[1]
    columns = weights_ref.shape[1]
    me, home = scalar_ref[sections], scalar_ref[sections + 1]
    count = batches * blocks
    own = pl.ds(pl.multiple_of(columns + home * count, count), count)
    kept = shared[0][own, :].astype(F32)
    for ref in shared[1:]:
        kept = kept * ref[own, :].astype(F32)
    kept_ref[...] = kept
    for k, ref in enumerate(shared):
        weights_ref[scalar_ref[k]] = ref[:columns, :]
    meta_ref[...] = jnp.zeros_like(meta_ref)
    meta_ref[:, :late, :] = jnp.full((owners, late, columns), -1.0, F32)
    buffer_ref[...] = jnp.zeros_like(buffer_ref)

    def visit(micro, block, owner, slot):
        at = owner ^ me if paired else owner
        meta_ref[at, pl.ds(FIELDS * late + slot, 1), :] = kept_ref[pl.ds(micro * blocks + block, 1), :]

        @pl.when(slot >= early)
        def _():
            lanes = pl.ds(pl.multiple_of(block * rows, rows), rows)
            source = (values_ref[micro * blocks + block], keys_ref[pl.ds(micro, 1), lanes], groups_ref[pl.ds(micro, 1), lanes])
            put_block(late, 0, source, at, slot - early, buffer_ref, meta_ref)

    walk_blocks(dest_ref, count_ref, owners, visit)
    buffer_ref[:, late * rows :, :] = meta_ref[...].astype(BF16)
    if len(outs) == 1:
        outs[0][...] = buffer_ref[...]
    else:
        for k, out in enumerate(outs):
            out[...] = buffer_ref[k]


def chain(values, weights):
    for weight in weights:
        half = jnp.dot(values, weight, preferred_element_type=F32) * 0.5
        values = (values.astype(F32) + (half + half * jnp.tanh(half))).astype(BF16)
    return values


def fetch_keys(meta_ref, start, slots, keys_ref, places_ref, sem):
    meta = meta_ref[:, start : start + 2 * slots, :].astype(F32)
    keys_ref[...] = (meta[:, :slots] * 128.0 + meta[:, slots:]).astype(I32)
    return pltpu.make_async_copy(keys_ref, places_ref, sem)


def find_rows(source, slots, at, rows, places_ref, table_ref, found_ref):
    for slot in range(slots):
        for row in range(rows):
            place = places_ref[source, slot, row]
            found_ref[pl.ds(at + slot * rows + row, 1), :] = table_ref[pl.ds(place, 1), :]


def join_first(slots, first_ref, weights_ref, table_ref, out_ref, keys_ref, found_ref, places_ref, sem):
    owners, columns = first_ref.shape[0], first_ref.shape[2]
    span = out_ref.shape[1]
    group = found_ref.shape[0] // span
    copy = fetch_keys(first_ref, span, slots, keys_ref, places_ref, sem)
    copy.start()
    weights = [weights_ref[j] for j in range(weights_ref.shape[0])]
    copy.wait()

    def step(turn, carry):
        base = turn * group
        values = first_ref[pl.ds(base, group), :span, :].reshape(group * span, columns)
        for source in range(group):
            find_rows(base + source, slots, source * span, span // slots, places_ref, table_ref, found_ref)
        joined = (chain(values, weights).astype(F32) * found_ref[...]).astype(BF16)
        out_ref[pl.ds(base, group)] = joined.reshape(group, span, columns)
        return carry

    lax.fori_loop(0, owners // group, step, 0)


def join_last(few, early, late, scalar_ref, first_ref, joined_ref, weights_ref, table_ref, *refs):
    parts, (out_ref, buffer_ref, meta_ref, keys_ref, found_ref, places_ref, list_ref, sem) = refs[:-8], refs[-8:]
    owners, span, columns = joined_ref.shape
    groups = out_ref.shape[0]
    rows = span // early
    batch = found_ref.shape[0] // rows
    me = scalar_ref[weights_ref.shape[0]]
    if few:
        for k, part in enumerate(parts):
            buffer_ref[me ^ k] = part[...]
    else:
        buffer_ref[...] = parts[0][...]
    copy = fetch_keys(buffer_ref, late * rows, late, keys_ref, places_ref, sem)
    copy.start()
    meta_ref[...] = buffer_ref[:, late * rows :, :].astype(F32)
    weights = [weights_ref[j] for j in range(weights_ref.shape[0])]
    sub = lax.broadcasted_iota(I32, (groups, rows), 0).astype(F32)
    step_size = math.gcd(owners, 8) if groups <= 128 else 1

    def early_step(turn, total):
        base = turn * step_size
        hot = []
        for source in range(step_size):
            meta = first_ref[base + source, span:, :].astype(F32)
            group = meta[2 * early : 3 * early] * 128.0 + meta[3 * early : 4 * early]
            group = jnp.where(meta_ref[base + source, FIELDS * late : FIELDS * late + early, :] > 0.5, group, -1.0)
            hot += [jnp.where(sub == group[j : j + 1], 1.0, 0.0).astype(BF16) for j in range(early)]
        joined = joined_ref[pl.ds(base, step_size)].reshape(step_size * span, columns)
        out_ref[...] += jnp.dot(jnp.concatenate(hot, axis=1), joined, preferred_element_type=F32)
        return total

    out_ref[...] = jnp.zeros_like(out_ref)
    lax.fori_loop(0, owners // step_size, early_step, 0)
    copy.wait()

    def note(source, count):
        for slot in range(late):
            list_ref[count] = source * late + slot
            count = count + jnp.where(places_ref[source, slot, 0] >= 0, 1, 0)
        return count

    filled = lax.fori_loop(0, owners, note, 0, unroll=min(owners, 8))

    def step(turn, carry):
        base = turn * batch
        values, hot = [], []
        for k in range(batch):
            there = base + k < filled
            item = list_ref[jnp.where(there, base + k, base)]
            source, slot = item // late, item % late
            values.append(buffer_ref[source, pl.ds(pl.multiple_of(slot * rows, rows), rows), :])
            group = meta_ref[source, pl.ds(2 * late + slot, 1), :] * 128.0 + meta_ref[source, pl.ds(3 * late + slot, 1), :]
            kept = meta_ref[source, pl.ds(FIELDS * late + early + slot, 1), :]
            group = jnp.where((kept > 0.5) & there, group, -1.0)
            hot.append(jnp.where(sub == group, 1.0, 0.0).astype(BF16))
            for row in range(rows):
                found_ref[k * rows + row : k * rows + row + 1, :] = table_ref[pl.ds(places_ref[source, slot, row], 1), :]
        joined = (chain(jnp.concatenate(values, axis=0), weights).astype(F32) * found_ref[...]).astype(BF16)
        out_ref[...] += jnp.dot(jnp.concatenate(hot, axis=1), joined, preferred_element_type=F32)
        return carry

    lax.fori_loop(0, (filled + batch - 1) // batch, step, 0)


def few_owners(owners):
    return owners <= 8 and owners & (owners - 1) == 0


def far_first(owners):
    return sorted(range(1, owners), key=lambda k: (-(k // (owners // 2)), -(k // 2), k))


def unpack_bits(bit_words):
    shifts = jnp.arange(16, dtype=jnp.int32)
    spread = jnp.right_shift(bit_words[..., None], shifts) & 1
    return spread.reshape(bit_words.shape[:-1] + (bit_words.shape[-1] * 16,))


def local(
    probe_values,
    probe_keys,
    group_ids,
    block_dest,
    filter_bits,
    section_weights,
    build_keys,
    build_values,
):
    sections = lax.axis_size("section")
    owners = lax.axis_size("owner")
    home = lax.axis_index("section").astype(I32)
    batches, block_count = block_dest.shape[:2]
    columns = probe_values.shape[2]
    rows = probe_values.shape[1] // block_count
    groups_all = GRP_DEV * sections * owners
    slots = batches * CAP
    late = slots // 2
    early = slots - late
    tile = 8
    early_meta = -(-FIELDS * early // tile) * tile
    late_meta = -(-(FIELDS * late + slots) // tile) * tile

    dest = block_dest.reshape(batches, block_count)
    blocks = probe_values.reshape(batches * block_count, rows, columns)
    counts = pltpu.SMEM((owners,), I32)
    first = run(
        functools.partial(pack_first, early),
        [dest, blocks, probe_keys, group_ids],
        ((owners, early * rows + early_meta, columns), BF16),
        [
            pltpu.SMEM(dest.shape, I32),
            pltpu.VMEM(blocks.shape, BF16),
            pltpu.VMEM(probe_keys.shape, I32),
            pltpu.VMEM(group_ids.shape, I32),
            pltpu.VMEM((owners, early_meta, columns), F32),
            counts,
            pltpu.SemaphoreType.DMA((4,)),
        ],
        away=True,
    )
    first = lax.all_to_all(first, "owner", split_axis=0, concat_axis=0, tiled=True)

    bits = unpack_bits(filter_bits[0]).astype(BF16).reshape(-1, rows)
    shared = jnp.concatenate([section_weights[0], bits], axis=0)
    paired = sections & (sections - 1) == 0

    def partner(index, k):
        return index ^ k if paired else (index - k) % sections

    received = [shared] + [
        lax.ppermute(shared, "section", [(partner(i, k), i) for i in range(sections)]) for k in range(1, sections)
    ]
    scalars = jnp.stack(
        [lax.rem(partner(home, k) - home + sections, sections) for k in range(sections)]
        + [lax.axis_index("owner").astype(I32), home]
    )
    table = run(
        build_table,
        [build_keys.reshape(-1, 128), build_values],
        ((KEYS_OWN, columns), F32),
        [pltpu.VMEM((build_values.shape[0], 2 * columns), BF16)],
        flops=2 * KEYS_OWN * build_keys.shape[0] * columns,
    )
    few = few_owners(owners)
    part = (late * rows + late_meta, columns)
    weights, *parts = run(
        functools.partial(pack_last, sections, few, early, late),
        [scalars] + received + [blocks, probe_keys, group_ids, dest],
        [((sections, columns, columns), BF16)] + ([(part, BF16)] * owners if few else [((owners, *part), BF16)]),
        [
            pltpu.VMEM((owners, *part), BF16),
            pltpu.VMEM((owners, late_meta, columns), F32),
            pltpu.VMEM((batches * block_count, rows), F32),
            counts,
        ],
        scalars=(0, 1 + sections + 3),
    )
    if few:
        for k in far_first(owners):
            parts[k] = lax.ppermute(parts[k], "owner", [(i, i ^ k) for i in range(owners)])
    else:
        parts = [lax.all_to_all(parts[0], "owner", split_axis=0, concat_axis=0, tiled=True)]

    group = math.gcd(owners, 4)
    joined = run(
        functools.partial(join_first, early),
        [first, weights, table],
        ((owners, early * rows, columns), BF16),
        [
            pltpu.VMEM((owners, early, rows), I32),
            pltpu.VMEM((group * early * rows, columns), F32),
            pltpu.SMEM((owners, early, rows), I32),
            pltpu.SemaphoreType.DMA,
        ],
        flops=2 * KEYS_OWN * owners * early * rows * columns,
    )
    sums = run(
        functools.partial(join_last, few, early, late),
        [scalars, first, joined, weights, table] + parts,
        ((groups_all, columns), F32),
        [
            pltpu.VMEM((owners, *part), BF16),
            pltpu.VMEM((owners, late_meta, columns), F32),
            pltpu.VMEM((owners, late, rows), I32),
            pltpu.VMEM((4 * rows, columns), F32),
            pltpu.SMEM((owners, late, rows), I32),
            pltpu.SMEM((owners * late + 1,), I32),
            pltpu.SemaphoreType.DMA,
        ],
        scalars=(0,),
        flops=2 * groups_all * owners * slots * rows * columns,
    )
    parts = sums.reshape(sections * owners, GRP_DEV, columns)
    parts = lax.all_to_all(parts, ("section", "owner"), split_axis=0, concat_axis=0, tiled=True)
    return jnp.sum(parts, axis=0)


def solution(mesh):
    placed = (
        P("section", "owner", None),
        P("section", "owner"),
        P("section", "owner"),
        P("section", "owner", None),
        P("section", None, "owner"),
        P("section", None, None),
        P("owner"),
        P("owner", None),
    )
    return jax.shard_map(
        local, mesh=mesh, in_specs=placed, out_specs=P(("section", "owner"), None), check_vma=False
    )
```

profile of v0, /device:TPU:0, one launch (start us, length us, event | category | flops | bytes accessed | tf_op | source)
XLA Modules:
  0.0 54.0 jit_solution(17507622214473819043)
XLA Ops:
  0.0 2.1 %shard_map.82 = bf16[8,264,128]{2,1,0:T(8,128)(2,1)} custom-call(s32[2,8]{1,0:T(2,128)} %bitcast.20, bf16[16,128,128]{2,1,0:T(8,128)(2,1)} %bitcast.17, s32[2,1024]{1,0:T(2,128)} %refs_5_.1, s32[2,1024]{1,0:T(2,128)} %refs_6_.1), custom_call_target="tpu_custom_call" | custom-call | tf_op jit(solution)/shard_map/pallas_call | solution.py:30
  2.1 6.5 %all-to-all-start = ((bf16[8,264,128]{2,1,0:T(8,128)(2,1)}), bf16[8,264,128]{2,1,0:T(8,128)(2,1)S(1)}, u32[]{:S(2)}, u32[]{:S(2)}) async-start(bf16[8,264,128]{2,1,0:T(8,128)(2,1)} %shard_map.82), calls=%async_computation | async-start | bytes 1081344 | tf_op jit(solution)/shard_map/all_to_all | solution.py:324
  8.7 0.1 shift_right_arithmetic.26
  8.9 0.1 shift_right_arithmetic.27
  9.0 0.7 %copy-done.6 = bf16[1,128,128]{2,1,0:T(8,128)(2,1)S(1)} copy-done((bf16[1,128,128]{2,1,0:T(8,128)(2,1)S(1)}, bf16[1,128,128]{2,1,0:T(8,128)(2,1)}, u32[]{:S(2)}) %copy-start.6) | copy-done | bytes 32792
  9.8 2.5 %collective-permute-start.2 = (bf16[192,128]{1,0:T(8,128)(2,1)S(1)}, bf16[192,128]{1,0:T(8,128)(2,1)S(1)}, u32[]{:S(2)}, u32[]{:S(2)}) collective-permute-start(bf16[192,128]{1,0:T(8,128)(2,1)S(1)} %pad_maximum_fusion.refs_0_), channel_id=1, source_target_pairs={{24,0},{16,8},{8,16},{0,24},{25,1},{17,9},{9,17},{1,25},{26,2},{18... | collective-permute-start | bytes 147464 | tf_op jit(solution)/shard_map/ppermute | solution.py:334
  12.2 0.5 collective-permute-start.1
  12.7 0.5 collective-permute-start
  13.3 0.1 stack.23.scalar_ref
  13.3 1.5 %collective-permute-done.2.refs_3_ = bf16[192,128]{1,0:T(8,128)(2,1)S(1)} collective-permute-done((bf16[192,128]{1,0:T(8,128)(2,1)S(1)}, bf16[192,128]{1,0:T(8,128)(2,1)S(1)}, u32[]{:S(2)}, u32[]{:S(2)}) %collective-permute-start.2) | collective-permute-done | bytes 49184 | tf_op jit(solution)/shard_map/ppermute | solution.py:334
  14.8 1.5 %collective-permute-done.1.refs_2_ = bf16[192,128]{1,0:T(8,128)(2,1)S(1)} collective-permute-done((bf16[192,128]{1,0:T(8,128)(2,1)S(1)}, bf16[192,128]{1,0:T(8,128)(2,1)S(1)}, u32[]{:S(2)}, u32[]{:S(2)}) %collective-permute-start.1) | collective-permute-done | bytes 49184 | tf_op jit(solution)/shard_map/ppermute | solution.py:334
  16.3 0.5 collective-permute-done.refs_1_
  16.8 1.6 %shard_map.83 = (bf16[4,128,128]{2,1,0:T(8,128)(2,1)S(1)}, bf16[272,128]{1,0:T(8,128)(2,1)S(1)}, bf16[272,128]{1,0:T(8,128)(2,1)S(1)}, bf16[272,128]{1,0:T(8,128...) custom-call(s32[6]{0:T(128)S(1)} %stack.23.scalar_ref, ...), custom_call_target="tpu_custom_call" | custom-call | tf_op jit(solution)/shard_map/pallas_call | solution.py:30
  18.4 2.0 %collective-permute-start.4 = (bf16[272,128]{1,0:T(8,128)(2,1)S(1)}, bf16[272,128]{1,0:T(8,128)(2,1)S(1)}, u32[]{:S(2)}, u32[]{:S(2)}) collective-permute-start(bf16[272,128]{1,0:T(8,128)(2,1)S(1)} %get-tuple-element.17), channel_id=1, source_target_pairs={{0,2},{1,3},{2,0},{3,1},{4,6},{5,7},{6,4},{7,5},{8,10},{9,11},{10,... | collective-permute-start | bytes 208904 | tf_op jit(solution)/shard_map/ppermute | solution.py:363
  20.4 4.2 %shard_map.84.table_ref = f32[2048,128]{1,0:T(8,128)S(1)} custom-call(s32[32,128]{1,0:T(8,128)S(1)} %bitcast.22, bf16[4096,128]{1,0:T(8,128)(2,1)S(1)} %copy-done.4), custom_call_target="tpu_custom_call" | custom-call | flops 2147483648 | bytes 10502144 | tf_op jit(solution)/shard_map/pallas_call | solution.py:30
  24.7 0.2 collective-permute-start.5
  24.8 2.6 %collective-permute-start.6 = (bf16[272,128]{1,0:T(8,128)(2,1)}, bf16[272,128]{1,0:T(8,128)(2,1)S(1)}, u32[]{:S(2)}, u32[]{:S(2)}) collective-permute-start(bf16[272,128]{1,0:T(8,128)(2,1)} %get-tuple-element.19), channel_id=1, source_target_pairs={{0,4},{1,5},{2,6},{3,7},{4,0},{5,1},{6,2},{7,3},{8,12},{9,13},{10,... | collective-permute-start | bytes 208904 | tf_op jit(solution)/shard_map/ppermute | solution.py:363
  27.5 3.4 %collective-permute-start.8 = (bf16[272,128]{1,0:T(8,128)(2,1)S(1)}, bf16[272,128]{1,0:T(8,128)(2,1)S(1)}, u32[]{:S(2)}, u32[]{:S(2)}) collective-permute-start(bf16[272,128]{1,0:T(8,128)(2,1)S(1)} %get-tuple-element.21), channel_id=1, source_target_pairs={{0,6},{1,7},{2,4},{3,5},{4,2},{5,3},{6,0},{7,1},{8,14},{9,15},{10,... | collective-permute-start | bytes 208904 | tf_op jit(solution)/shard_map/ppermute | solution.py:363
  30.9 0.2 collective-permute-start.9
  31.1 3.7 %shard_map.85.joined_ref = bf16[8,256,128]{2,1,0:T(8,128)(2,1)S(1)} custom-call(bf16[8,264,128]{2,1,0:T(8,128)(2,1)S(1)} %all-to-all-done.first_ref, bf16[4,128,128]{2,1,0:T(8,128)(2,1)S(1)} %get-tuple-element.14.weights_ref, f32[2048,128]{1,0:T(8,128)S(1)} %shard_map.84.table_ref), custom_call_target="tpu_custom_call" | custom-call | flops 1073741824 | bytes 3325960 | tf_op jit(solution)/shard_map/pallas_call | solution.py:30
  34.8 3.7 %collective-permute-done.7.refs_5_ = bf16[272,128]{1,0:T(8,128)(2,1)S(1)} collective-permute-done((bf16[272,128]{1,0:T(8,128)(2,1)S(1)}, bf16[272,128]{1,0:T(8,128)(2,1)S(1)}, u32[]{:S(2)}, u32[]{:S(2)}) %collective-permute-start.7) | collective-permute-done | bytes 69664 | tf_op jit(solution)/shard_map/ppermute | solution.py:363
  38.5 1.6 %shard_map.86 = f32[128,128]{1,0:T(8,128)S(1)} custom-call(s32[6]{0:T(128)S(1)} %stack.23.scalar_ref, bf16[8,264,128]{2,1,0:T(8,128)(2,1)S(1)} %all-to-all-done.first_ref, bf16[8,256,128]{2,1,0:T(8,128)(2,1)S(1)} %shard_map.85.joined_ref, bf16[4,128,128]{2,1,0:T(8,128)(2,1)S(1)} %get-tuple-element.14.weights_ref, f32[2048,128]{1,0:T(8,128)S(1)} %shard_map.84.table_ref, ...), custom_call_target="tpu_custom_call" | custom-call | flops 134217728 | bytes 5783696 | tf_op jit(solution)/shard_map/pallas_call | solution.py:30
  40.0 13.3 %all_to_all.10 = f32[32,4,128]{2,1,0:T(4,128)S(1)} all-to-all(f32[32,4,128]{2,1,0:T(4,128)S(1)} %bitcast.19), channel_id=1, replica_groups=mesh['section'=4,'owner'=8] {'section','owner'}, dimensions={0} | all-to-all | bytes 131072 | tf_op jit(solution)/shard_map/all_to_all | solution.py:397
  53.4 0.6 %reduce_sum.9 = f32[4,128]{1,0:T(4,128)} reduce(f32[32,4,128]{2,1,0:T(4,128)S(1)} %all_to_all.10, f32[]{:T(128)} %constant.27.clone.1), dimensions={0}, to_apply=%region_0.0 | reduce | flops 15872 | bytes 67588 | tf_op jit(solution)/shard_map/reduce_sum | solution.py:398
  (28 shorter events, 0.2 us)
Async XLA Ops:
  2.1 6.6 %copy-start.7 = (s32[1,8,64]{2,1,0:T(8,128)S(1)}, s32[1,8,64]{2,1,0:T(8,128)}, u32[]{:S(2)}) copy-start(s32[1,8,64]{2,1,0:T(8,128)} %param.12) | copy-start | bytes 6148
  2.1 18.3 %copy-start.4 = (bf16[4096,128]{1,0:T(8,128)(2,1)S(1)}, bf16[4096,128]{1,0:T(8,128)(2,1)}, u32[]{:S(2)}) copy-start(bf16[4096,128]{1,0:T(8,128)(2,1)} %values_ref.1) | copy-start | bytes 3145732
  2.1 29.0 %all-to-all-start = ((bf16[8,264,128]{2,1,0:T(8,128)(2,1)}), bf16[8,264,128]{2,1,0:T(8,128)(2,1)S(1)}, u32[]{:S(2)}, u32[]{:S(2)}) async-start(bf16[8,264,128]{2,1,0:T(8,128)(2,1)} %shard_map.82), calls=%async_computation | async-start | bytes 1081344 | tf_op jit(solution)/shard_map/all_to_all | solution.py:324
  8.6 8.2 %copy-start = (bf16[2,1024,128]{2,1,0:T(8,128)(2,1)S(1)}, bf16[2,1024,128]{2,1,0:T(8,128)(2,1)}, u32[]{:S(2)}) copy-start(bf16[2,1024,128]{2,1,0:T(8,128)(2,1)} %param.8) | copy-start | bytes 1572868
  9.0 0.8 %copy-start.6 = (bf16[1,128,128]{2,1,0:T(8,128)(2,1)S(1)}, bf16[1,128,128]{2,1,0:T(8,128)(2,1)}, u32[]{:S(2)}) copy-start(bf16[1,128,128]{2,1,0:T(8,128)(2,1)} %param.13) | copy-start | bytes 98308
  9.8 5.0 %collective-permute-start.2 = (bf16[192,128]{1,0:T(8,128)(2,1)S(1)}, bf16[192,128]{1,0:T(8,128)(2,1)S(1)}, u32[]{:S(2)}, u32[]{:S(2)}) collective-permute-start(bf16[192,128]{1,0:T(8,128)(2,1)S(1)} %pad_maximum_fusion.refs_0_), channel_id=1, source_target_pairs={{24,0},{16,8},{8,16},{0,24},{25,1},{17,9},{9,17},{1,25},{26,2},{18... | collective-permute-start | bytes 147464 | tf_op jit(solution)/shard_map/ppermute | solution.py:334
  12.2 4.1 %collective-permute-start.1 = (bf16[192,128]{1,0:T(8,128)(2,1)S(1)}, bf16[192,128]{1,0:T(8,128)(2,1)S(1)}, u32[]{:S(2)}, u32[]{:S(2)}) collective-permute-start(bf16[192,128]{1,0:T(8,128)(2,1)S(1)} %pad_maximum_fusion.refs_0_), channel_id=1, source_target_pairs={{16,0},{24,8},{0,16},{8,24},{17,1},{25,9},{1,17},{9,25},{18,2},{26... | collective-permute-start | bytes 147464 | tf_op jit(solution)/shard_map/ppermute | solution.py:334
  12.7 4.1 %collective-permute-start = (bf16[192,128]{1,0:T(8,128)(2,1)S(1)}, bf16[192,128]{1,0:T(8,128)(2,1)S(1)}, u32[]{:S(2)}, u32[]{:S(2)}) collective-permute-start(bf16[192,128]{1,0:T(8,128)(2,1)S(1)} %pad_maximum_fusion.refs_0_), channel_id=1, source_target_pairs={{8,0},{0,8},{24,16},{16,24},{9,1},{1,9},{25,17},{17,25},{10,2},{2,... | collective-permute-start | bytes 147464 | tf_op jit(solution)/shard_map/ppermute | solution.py:334
  13.2 3.6 %copy-start.3 = (s32[2,8,1]{1,2,0:T(1,128)S(1)}, s32[2,8,1]{1,2,0:T(1,128)}, u32[]{:S(2)}) copy-start(s32[2,8,1]{1,2,0:T(1,128)} %param.11) | copy-start | bytes 196
  13.2 3.6 %copy-start.1 = (s32[2,1024]{1,0:T(2,128)S(1)}, s32[2,1024]{1,0:T(2,128)}, u32[]{:S(2)}) copy-start(s32[2,1024]{1,0:T(2,128)} %refs_5_.1) | copy-start | bytes 24580
  13.3 3.6 %copy-start.2 = (s32[2,1024]{1,0:T(2,128)S(1)}, s32[2,1024]{1,0:T(2,128)}, u32[]{:S(2)}) copy-start(s32[2,1024]{1,0:T(2,128)} %refs_6_.1) | copy-start | bytes 24580
  13.3 7.1 %copy-start.5 = (s32[4096]{0:T(1024)S(1)}, s32[4096]{0:T(1024)}, u32[]{:S(2)}) copy-start(s32[4096]{0:T(1024)} %param.14) | copy-start | bytes 49156
  18.4 9.1 %collective-permute-start.3 = (bf16[272,128]{1,0:T(8,128)(2,1)S(1)}, bf16[272,128]{1,0:T(8,128)(2,1)S(1)}, u32[]{:S(2)}, u32[]{:S(2)}) collective-permute-start(bf16[272,128]{1,0:T(8,128)(2,1)S(1)} %get-tuple-element.16), channel_id=1, source_target_pairs={{0,1},{1,0},{2,3},{3,2},{4,5},{5,4},{6,7},{7,6},{8,9},{9,8},{10,11... | collective-permute-start | bytes 208904 | tf_op jit(solution)/shard_map/ppermute | solution.py:363
  18.4 12.5 %collective-permute-start.4 = (bf16[272,128]{1,0:T(8,128)(2,1)S(1)}, bf16[272,128]{1,0:T(8,128)(2,1)S(1)}, u32[]{:S(2)}, u32[]{:S(2)}) collective-permute-start(bf16[272,128]{1,0:T(8,128)(2,1)S(1)} %get-tuple-element.17), channel_id=1, source_target_pairs={{0,2},{1,3},{2,0},{3,1},{4,6},{5,7},{6,4},{7,5},{8,10},{9,11},{10,... | collective-permute-start | bytes 208904 | tf_op jit(solution)/shard_map/ppermute | solution.py:363
  24.7 10.1 %collective-permute-start.5 = (bf16[272,128]{1,0:T(8,128)(2,1)}, bf16[272,128]{1,0:T(8,128)(2,1)S(1)}, u32[]{:S(2)}, u32[]{:S(2)}) collective-permute-start(bf16[272,128]{1,0:T(8,128)(2,1)} %get-tuple-element.18), channel_id=1, source_target_pairs={{0,3},{1,2},{2,1},{3,0},{4,7},{5,6},{6,5},{7,4},{8,11},{9,10},{10,... | collective-permute-start | bytes 208904 | tf_op jit(solution)/shard_map/ppermute | solution.py:363
  24.8 9.9 %collective-permute-start.6 = (bf16[272,128]{1,0:T(8,128)(2,1)}, bf16[272,128]{1,0:T(8,128)(2,1)S(1)}, u32[]{:S(2)}, u32[]{:S(2)}) collective-permute-start(bf16[272,128]{1,0:T(8,128)(2,1)} %get-tuple-element.19), channel_id=1, source_target_pairs={{0,4},{1,5},{2,6},{3,7},{4,0},{5,1},{6,2},{7,3},{8,12},{9,13},{10,... | collective-permute-start | bytes 208904 | tf_op jit(solution)/shard_map/ppermute | solution.py:363
  27.5 11.0 %collective-permute-start.7 = (bf16[272,128]{1,0:T(8,128)(2,1)S(1)}, bf16[272,128]{1,0:T(8,128)(2,1)S(1)}, u32[]{:S(2)}, u32[]{:S(2)}) collective-permute-start(bf16[272,128]{1,0:T(8,128)(2,1)S(1)} %get-tuple-element.20), channel_id=1, source_target_pairs={{0,5},{1,4},{2,7},{3,6},{4,1},{5,0},{6,3},{7,2},{8,13},{9,12},{10,... | collective-permute-start | bytes 208904 | tf_op jit(solution)/shard_map/ppermute | solution.py:363
  27.5 11.0 %collective-permute-start.8 = (bf16[272,128]{1,0:T(8,128)(2,1)S(1)}, bf16[272,128]{1,0:T(8,128)(2,1)S(1)}, u32[]{:S(2)}, u32[]{:S(2)}) collective-permute-start(bf16[272,128]{1,0:T(8,128)(2,1)S(1)} %get-tuple-element.21), channel_id=1, source_target_pairs={{0,6},{1,7},{2,4},{3,5},{4,2},{5,3},{6,0},{7,1},{8,14},{9,15},{10,... | collective-permute-start | bytes 208904 | tf_op jit(solution)/shard_map/ppermute | solution.py:363
  30.9 7.5 %collective-permute-start.9 = (bf16[272,128]{1,0:T(8,128)(2,1)S(1)}, bf16[272,128]{1,0:T(8,128)(2,1)S(1)}, u32[]{:S(2)}, u32[]{:S(2)}) collective-permute-start(bf16[272,128]{1,0:T(8,128)(2,1)S(1)} %get-tuple-element.22), channel_id=1, source_target_pairs={{0,7},{1,6},{2,5},{3,4},{4,3},{5,2},{6,1},{7,0},{8,15},{9,14},{10,... | collective-permute-start | bytes 208904 | tf_op jit(solution)/shard_map/ppermute | solution.py:363
where the time goes:
time: 54.3 us; the launch traced here: 54 us
  starting transfers between devices  18.4 us (34%)
  blocking collectives  13.3 us (24%)
  Pallas kernels  13.1 us (24%)
  waiting for transfers between devices  7.15 us (13%)
  local copies, waits for them, and re-layouts  1.19 us (2%)
  other arithmetic  0.63 us (1%)
    all_to_all x1, blocking collectives, local(): lax.all_to_all(parts, ('section', 'owner'), split_axis=0, concat_axis=0,...  13.3 us
    pallas_call x5, Pallas kernels, run(): pl.pallas_call(kernel, out_shape=shapes if several else shapes[0], in_spe...  13.1 us
    ppermute x7, starting transfers between devices, local(): lax.ppermute(parts[k], 'owner', [(i, i ^ k) for i in range(owners)])  8.46 us
    all_to_all x1, starting transfers between devices, local(): lax.all_to_all(first, 'owner', split_axis=0, concat_axis=0, tiled=True)  6.5 us
    ppermute x7, waiting for transfers between devices, local(): lax.ppermute(parts[k], 'owner', [(i, i ^ k) for i in range(owners)])  3.68 us
    ppermute x3, starting transfers between devices, local(): lax.ppermute(shared, 'section', [(partner(i, k), i) for i in range(sectio...  3.49 us
    ppermute x3, waiting for transfers between devices, local(): lax.ppermute(shared, 'section', [(partner(i, k), i) for i in range(sectio...  3.46 us
  transfers between devices with their start and end apart: 11, of which 4 were waited for; matrix products, arithmetic and copies ran while one was open for 1% of the time, Pallas kernels for 18%

commit v1 on v0

--- a/solution.py
+++ b/solution.py
@@ -12,7 +12,8 @@
 CAP = 2
 KEYS_OWN = 2048
 GRP_DEV = 4
-FIELDS = 4
+FIELDS = 3
+MASKED = -16384.0
 BF16 = jnp.bfloat16
 F32 = jnp.float32
 I32 = jnp.int32
@@ -58,28 +59,59 @@
         lax.fori_loop(0, blocks, step, 0, unroll=min(blocks, 8))
 
 
-def put_block(slots, field_base, source, owner_at, slot, out_ref, meta_ref):
+def put_block(slots, source, kept, owner_at, slot, out_ref, meta_ref):
     values, keys, groups = source
     rows = values.shape[0]
     out_ref[owner_at, pl.ds(pl.multiple_of(slot * rows, rows), rows), :] = values
-    for field, part in enumerate((keys >> 7, keys & 127, groups >> 7, groups & 127)):
-        meta_ref[owner_at, pl.ds(field_base + field * slots + slot, 1), :] = part.astype(F32)
+    high = ((groups >> 7) * (KEYS_OWN // 128) + (keys >> 7)).astype(F32)
+    low = (groups & 127).astype(F32)
+    if kept is not None:
+        low = jnp.where(kept > 0.5, low, MASKED)
+    for field, part in enumerate((high, (keys & 127).astype(F32), low)):
+        meta_ref[owner_at, pl.ds(field * slots + slot, 1), :] = part
+
+
+def key_of(high, low):
+    return (high.astype(I32) & (KEYS_OWN // 128 - 1)) * 128 + low.astype(I32)
+
+
+def group_of(high, low):
+    return (high.astype(I32) // (KEYS_OWN // 128) * 128).astype(F32) + low
+
+
+def share_bits(words_ref, weight_ref, shared_ref):
+    columns = weight_ref.shape[0]
+    shared_ref[:columns, :] = weight_ref[...]
+    words = words_ref[...]
+    micros, length = words.shape
+    parts = jnp.concatenate([words & 255, words >> 8], axis=0).astype(F32).astype(BF16)
+    width = min(length, 128)
+    spread = lax.broadcasted_iota(I32, (width, width * 16), 1) // 16 == lax.broadcasted_iota(I32, (width, width * 16), 0)
+    spread = jnp.where(spread, 1.0, 0.0).astype(BF16)
+    place = lax.broadcasted_iota(I32, (micros, width * 16), 1) & 15
+    for turn in range(length // width):
+        found = jnp.dot(parts[:, turn * width : (turn + 1) * width], spread, preferred_element_type=F32).astype(I32)
+        bits = (jnp.where(place < 8, found[:micros], found[micros:]) >> (place & 7)) & 1
+        stacked = jnp.concatenate([bits[:, k : k + 128] for k in range(0, width * 16, 128)], axis=0)
+        start = columns + turn * stacked.shape[0]
+        shared_ref[start : start + stacked.shape[0], :] = stacked.astype(F32).astype(BF16)
 
 
 def pack_first(early, *refs):
-    sources, (out_ref, dest_ref, values_ref, keys_ref, groups_ref, meta_ref, count_ref, sems) = refs[:4], refs[4:]
+    sources, (out_ref, shared_ref), held, (meta_ref, count_ref, sems) = refs[:6], refs[6:8], refs[8:14], refs[14:]
+    dest_ref, values_ref, keys_ref, groups_ref, words_ref, weight_ref = held
     owners = out_ref.shape[0]
     blocks = dest_ref.shape[1]
     rows = values_ref.shape[1]
-    copies = [
-        pltpu.make_async_copy(source, target, sems.at[k])
-        for k, (source, target) in enumerate(zip(sources, (dest_ref, values_ref, keys_ref, groups_ref)))
-    ]
+    copies = [pltpu.make_async_copy(source, target, sems.at[k]) for k, (source, target) in enumerate(zip(sources, held))]
     for copy in copies:
         copy.start()
     meta_ref[...] = jnp.zeros_like(meta_ref)
     out_ref[...] = jnp.zeros_like(out_ref)
-    for copy in copies:
+    copies[4].wait()
+    copies[5].wait()
+    share_bits(words_ref, weight_ref, shared_ref)
+    for copy in copies[:4]:
         copy.wait()
 
     def visit(micro, block, owner, slot):
@@ -87,7 +119,7 @@
         def _():
             lanes = pl.ds(pl.multiple_of(block * rows, rows), rows)
             source = (values_ref[micro * blocks + block], keys_ref[pl.ds(micro, 1), lanes], groups_ref[pl.ds(micro, 1), lanes])
-            put_block(early, 0, source, owner, slot, out_ref, meta_ref)
+            put_block(early, source, None, owner, slot, out_ref, meta_ref)
 
     walk_blocks(dest_ref, count_ref, owners, visit)
     out_ref[:, early * rows :, :] = meta_ref[...].astype(BF16)
@@ -129,27 +161,29 @@
     rows = values_ref.shape[1]
     columns = weights_ref.shape[1]
     me, home = scalar_ref[sections], scalar_ref[sections + 1]
-    count = batches * blocks
-    own = pl.ds(pl.multiple_of(columns + home * count, count), count)
-    kept = shared[0][own, :].astype(F32)
+    kept = shared[0][columns:, :].astype(F32)
     for ref in shared[1:]:
-        kept = kept * ref[own, :].astype(F32)
+        kept = kept * ref[columns:, :].astype(F32)
     kept_ref[...] = kept
+    micros = kept.shape[0] // blocks
     for k, ref in enumerate(shared):
-        weights_ref[scalar_ref[k]] = ref[:columns, :]
+        weights_ref[scalar_ref[k]] = (ref[:columns, :].astype(F32) * 0.5).astype(BF16)
     meta_ref[...] = jnp.zeros_like(meta_ref)
-    meta_ref[:, :late, :] = jnp.full((owners, late, columns), -1.0, F32)
     buffer_ref[...] = jnp.zeros_like(buffer_ref)
 
     def visit(micro, block, owner, slot):
         at = owner ^ me if paired else owner
-        meta_ref[at, pl.ds(FIELDS * late + slot, 1), :] = kept_ref[pl.ds(micro * blocks + block, 1), :]
+        kept = kept_ref[pl.ds(block * micros + home * batches + micro, 1), :]
+
+        @pl.when(slot < early)
+        def _():
+            meta_ref[at, pl.ds(FIELDS * late + slot, 1), :] = kept
 
         @pl.when(slot >= early)
         def _():
             lanes = pl.ds(pl.multiple_of(block * rows, rows), rows)
             source = (values_ref[micro * blocks + block], keys_ref[pl.ds(micro, 1), lanes], groups_ref[pl.ds(micro, 1), lanes])
-            put_block(late, 0, source, at, slot - early, buffer_ref, meta_ref)
+            put_block(late, source, kept, at, slot - early, buffer_ref, meta_ref)
 
     walk_blocks(dest_ref, count_ref, owners, visit)
     buffer_ref[:, late * rows :, :] = meta_ref[...].astype(BF16)
@@ -162,107 +196,121 @@
 
 def chain(values, weights):
     for weight in weights:
-        half = jnp.dot(values, weight, preferred_element_type=F32) * 0.5
+        half = jnp.dot(values, weight, preferred_element_type=F32)
         values = (values.astype(F32) + (half + half * jnp.tanh(half))).astype(BF16)
     return values
 
 
-def fetch_keys(meta_ref, start, slots, keys_ref, places_ref, sem):
-    meta = meta_ref[:, start : start + 2 * slots, :].astype(F32)
-    keys_ref[...] = (meta[:, :slots] * 128.0 + meta[:, slots:]).astype(I32)
-    return pltpu.make_async_copy(keys_ref, places_ref, sem)
-
-
-def find_rows(source, slots, at, rows, places_ref, table_ref, found_ref):
-    for slot in range(slots):
+def join_rows(values, weights, rows, place_of, table_ref, found_ref):
+    count = values.shape[0] // rows
+    for block in range(count):
         for row in range(rows):
-            place = places_ref[source, slot, row]
-            found_ref[pl.ds(at + slot * rows + row, 1), :] = table_ref[pl.ds(place, 1), :]
+            found_ref[block * rows + row : block * rows + row + 1, :] = table_ref[pl.ds(place_of(block, row), 1), :]
+    return (chain(values, weights).astype(F32) * found_ref[...]).astype(BF16)
+
+
+def over(count, stride, step):
+    if count <= 8:
+        for base in range(0, count, stride):
+            step(base)
+    else:
+
+        def turn(k, carry):
+            step(k * stride)
+            return carry
+
+        lax.fori_loop(0, count // stride, turn, 0)
 
 
 def join_first(slots, first_ref, weights_ref, table_ref, out_ref, keys_ref, found_ref, places_ref, sem):
     owners, columns = first_ref.shape[0], first_ref.shape[2]
     span = out_ref.shape[1]
+    rows = span // slots
     group = found_ref.shape[0] // span
-    copy = fetch_keys(first_ref, span, slots, keys_ref, places_ref, sem)
+    meta = first_ref[:, span:, :].astype(F32)
+    keys_ref[...] = key_of(meta[:, :slots], meta[:, slots : 2 * slots])
+    copy = pltpu.make_async_copy(keys_ref, places_ref, sem)
     copy.start()
     weights = [weights_ref[j] for j in range(weights_ref.shape[0])]
     copy.wait()
 
-    def step(turn, carry):
-        base = turn * group
+    def step(base):
         values = first_ref[pl.ds(base, group), :span, :].reshape(group * span, columns)
-        for source in range(group):
-            find_rows(base + source, slots, source * span, span // slots, places_ref, table_ref, found_ref)
-        joined = (chain(values, weights).astype(F32) * found_ref[...]).astype(BF16)
+        joined = join_rows(
+            values,
+            weights,
+            rows,
+            lambda block, row: places_ref[base + block // slots, block % slots, row],
+            table_ref,
+            found_ref,
+        )
         out_ref[pl.ds(base, group)] = joined.reshape(group, span, columns)
-        return carry
-
-    lax.fori_loop(0, owners // group, step, 0)
+
+    over(owners, group, step)
 
 
 def join_last(few, early, late, scalar_ref, first_ref, joined_ref, weights_ref, table_ref, *refs):
-    parts, (out_ref, buffer_ref, meta_ref, keys_ref, found_ref, places_ref, list_ref, sem) = refs[:-8], refs[-8:]
-    owners, span, columns = joined_ref.shape
+    parts, (out_ref, keys_ref, found_ref, places_ref, sem) = refs[:-5], refs[-5:]
+    owners, span, _ = joined_ref.shape
     groups = out_ref.shape[0]
     rows = span // early
-    batch = found_ref.shape[0] // rows
+    late_span = late * rows
+    group = found_ref.shape[0] // late_span
     me = scalar_ref[weights_ref.shape[0]]
+
+    def part_of(k):
+        return parts[k] if few else parts[0].at[k]
+
     if few:
         for k, part in enumerate(parts):
-            buffer_ref[me ^ k] = part[...]
+            meta = part[late_span:, :].astype(F32)
+            keys_ref[k] = key_of(meta[:late], meta[late : 2 * late])
     else:
-        buffer_ref[...] = parts[0][...]
-    copy = fetch_keys(buffer_ref, late * rows, late, keys_ref, places_ref, sem)
+        meta = parts[0][:, late_span:, :].astype(F32)
+        keys_ref[...] = key_of(meta[:, :late], meta[:, late : 2 * late])
+    copy = pltpu.make_async_copy(keys_ref, places_ref, sem)
     copy.start()
-    meta_ref[...] = buffer_ref[:, late * rows :, :].astype(F32)
     weights = [weights_ref[j] for j in range(weights_ref.shape[0])]
     sub = lax.broadcasted_iota(I32, (groups, rows), 0).astype(F32)
-    step_size = math.gcd(owners, 8) if groups <= 128 else 1
-
-    def early_step(turn, total):
-        base = turn * step_size
+
+    def hot_rows(group_keys):
+        return [jnp.where(sub == group_keys[j : j + 1], 1.0, 0.0).astype(BF16) for j in range(group_keys.shape[0])]
+
+    out_ref[...] = jnp.zeros_like(out_ref)
+
+    def early_step(base):
+        hot, joined = [], []
+        for k in range(group):
+            source = me ^ (base + k) if few else base + k
+            meta = first_ref[source, span:, :].astype(F32)
+            kept = part_of(base + k)[late_span:, :].astype(F32)[FIELDS * late : FIELDS * late + early]
+            keys = group_of(meta[:early], meta[2 * early : 3 * early])
+            hot += hot_rows(jnp.where(kept > 0.5, keys, -1.0))
+            joined.append(joined_ref[source])
+        out_ref[...] += jnp.dot(
+            jnp.concatenate(hot, axis=1), jnp.concatenate(joined, axis=0), preferred_element_type=F32
+        )
+
+    over(owners, group, early_step)
+    copy.wait()
+
+    def step(base):
+        values = jnp.concatenate([part_of(base + k)[:late_span, :] for k in range(group)], axis=0)
         hot = []
-        for source in range(step_size):
-            meta = first_ref[base + source, span:, :].astype(F32)
-            group = meta[2 * early : 3 * early] * 128.0 + meta[3 * early : 4 * early]
-            group = jnp.where(meta_ref[base + source, FIELDS * late : FIELDS * late + early, :] > 0.5, group, -1.0)
-            hot += [jnp.where(sub == group[j : j + 1], 1.0, 0.0).astype(BF16) for j in range(early)]
-        joined = joined_ref[pl.ds(base, step_size)].reshape(step_size * span, columns)
+        for k in range(group):
+            meta = part_of(base + k)[late_span:, :].astype(F32)
+            hot += hot_rows(group_of(meta[:late], meta[2 * late : 3 * late]))
+        joined = join_rows(
+            values,
+            weights,
+            rows,
+            lambda block, row: places_ref[base + block // late, block % late, row],
+            table_ref,
+            found_ref,
+        )
         out_ref[...] += jnp.dot(jnp.concatenate(hot, axis=1), joined, preferred_element_type=F32)
-        return total
-
-    out_ref[...] = jnp.zeros_like(out_ref)
-    lax.fori_loop(0, owners // step_size, early_step, 0)
-    copy.wait()
-
-    def note(source, count):
-        for slot in range(late):
-            list_ref[count] = source * late + slot
-            count = count + jnp.where(places_ref[source, slot, 0] >= 0, 1, 0)
-        return count
-
-    filled = lax.fori_loop(0, owners, note, 0, unroll=min(owners, 8))
-
-    def step(turn, carry):
-        base = turn * batch
-        values, hot = [], []
-        for k in range(batch):
-            there = base + k < filled
-            item = list_ref[jnp.where(there, base + k, base)]
-            source, slot = item // late, item % late
-            values.append(buffer_ref[source, pl.ds(pl.multiple_of(slot * rows, rows), rows), :])
-            group = meta_ref[source, pl.ds(2 * late + slot, 1), :] * 128.0 + meta_ref[source, pl.ds(3 * late + slot, 1), :]
-            kept = meta_ref[source, pl.ds(FIELDS * late + early + slot, 1), :]
-            group = jnp.where((kept > 0.5) & there, group, -1.0)
-            hot.append(jnp.where(sub == group, 1.0, 0.0).astype(BF16))
-            for row in range(rows):
-                found_ref[k * rows + row : k * rows + row + 1, :] = table_ref[pl.ds(places_ref[source, slot, row], 1), :]
-        joined = (chain(jnp.concatenate(values, axis=0), weights).astype(F32) * found_ref[...]).astype(BF16)
-        out_ref[...] += jnp.dot(jnp.concatenate(hot, axis=1), joined, preferred_element_type=F32)
-        return carry
-
-    lax.fori_loop(0, (filled + batch - 1) // batch, step, 0)
+
+    over(owners, group, step)
 
 
 def few_owners(owners):
@@ -271,12 +319,6 @@
 
 def far_first(owners):
     return sorted(range(1, owners), key=lambda k: (-(k // (owners // 2)), -(k // 2), k))
-
-
-def unpack_bits(bit_words):
-    shifts = jnp.arange(16, dtype=jnp.int32)
-    spread = jnp.right_shift(bit_words[..., None], shifts) & 1
-    return spread.reshape(bit_words.shape[:-1] + (bit_words.shape[-1] * 16,))
 
 
 def local(
@@ -301,30 +343,26 @@
     early = slots - late
     tile = 8
     early_meta = -(-FIELDS * early // tile) * tile
-    late_meta = -(-(FIELDS * late + slots) // tile) * tile
+    late_meta = -(-(FIELDS * late + early) // tile) * tile
 
     dest = block_dest.reshape(batches, block_count)
     blocks = probe_values.reshape(batches * block_count, rows, columns)
     counts = pltpu.SMEM((owners,), I32)
-    first = run(
+    words = filter_bits[0]
+    micros = words.shape[0]
+    shared_shape = (columns + micros * block_count, columns)
+    sources = [dest, blocks, probe_keys, group_ids, words, section_weights[0]]
+    first, shared = run(
         functools.partial(pack_first, early),
-        [dest, blocks, probe_keys, group_ids],
-        ((owners, early * rows + early_meta, columns), BF16),
-        [
-            pltpu.SMEM(dest.shape, I32),
-            pltpu.VMEM(blocks.shape, BF16),
-            pltpu.VMEM(probe_keys.shape, I32),
-            pltpu.VMEM(group_ids.shape, I32),
-            pltpu.VMEM((owners, early_meta, columns), F32),
-            counts,
-            pltpu.SemaphoreType.DMA((4,)),
-        ],
+        sources,
+        [((owners, early * rows + early_meta, columns), BF16), (shared_shape, BF16)],
+        [pltpu.SMEM(dest.shape, I32)]
+        + [pltpu.VMEM(source.shape, source.dtype) for source in sources[1:]]
+        + [pltpu.VMEM((owners, early_meta, columns), F32), counts, pltpu.SemaphoreType.DMA((len(sources),))],
         away=True,
     )
     first = lax.all_to_all(first, "owner", split_axis=0, concat_axis=0, tiled=True)
 
-    bits = unpack_bits(filter_bits[0]).astype(BF16).reshape(-1, rows)
-    shared = jnp.concatenate([section_weights[0], bits], axis=0)
     paired = sections & (sections - 1) == 0
 
     def partner(index, k):
@@ -353,7 +391,7 @@
         [
             pltpu.VMEM((owners, *part), BF16),
             pltpu.VMEM((owners, late_meta, columns), F32),
-            pltpu.VMEM((batches * block_count, rows), F32),
+            pltpu.VMEM((micros * block_count, rows), F32),
             counts,
         ],
         scalars=(0, 1 + sections + 3),
@@ -382,12 +420,9 @@
         [scalars, first, joined, weights, table] + parts,
         ((groups_all, columns), F32),
         [
-            pltpu.VMEM((owners, *part), BF16),
-            pltpu.VMEM((owners, late_meta, columns), F32),
             pltpu.VMEM((owners, late, rows), I32),
-            pltpu.VMEM((4 * rows, columns), F32),
+            pltpu.VMEM((group * late * rows, columns), F32),
             pltpu.SMEM((owners, late, rows), I32),
-            pltpu.SMEM((owners * late + 1,), I32),
             pltpu.SemaphoreType.DMA,
         ],
         scalars=(0,),

time: 54.3 us -> 55.5 us (1.022)
  Pallas kernels: 13.1 us -> 14.9 us
  local copies, waits for them, and re-layouts: 1.19 us -> 0.11 us
  waiting for transfers between devices: 7.15 us -> 7.82 us
    pallas_call x5, Pallas kernels: 13.1 us -> 14.9 us  [run(): pl.pallas_call(kernel, out_shape=shapes if several else shapes[0], in_spe...]
    unnamed x16 -> x14, local copies, waits for them, and re-layouts: 0.77 us -> 0.03 us
    ppermute x7, waiting for transfers between devices: 3.68 us -> 4.35 us  [local(): lax.ppermute(parts[k], 'owner', [(i, i ^ k) for i in range(owners)])]
  transfers between devices with their start and end apart: 11 -> 11, of which waited for: 4 -> 4; matrix products, arithmetic and copies ran while one was open for 1% -> 0% of each run, Pallas kernels for 18% -> 16%
where the time goes in v1:
time: 55.5 us; the launch traced here: 55.2 us
  starting transfers between devices  18.4 us (33%)
  Pallas kernels  14.9 us (27%)
  blocking collectives  13.2 us (24%)
  waiting for transfers between devices  7.82 us (14%)
  other arithmetic  0.62 us (1%)
    pallas_call x5, Pallas kernels, run(): pl.pallas_call(kernel, out_shape=shapes if several else shapes[0], in_spe...  14.9 us
    all_to_all x1, blocking collectives, local(): lax.all_to_all(parts, ('section', 'owner'), split_axis=0, concat_axis=0,...  13.2 us
    ppermute x7, starting transfers between devices, local(): lax.ppermute(parts[k], 'owner', [(i, i ^ k) for i in range(owners)])  8.4 us
    all_to_all x1, starting transfers between devices, local(): lax.all_to_all(first, 'owner', split_axis=0, concat_axis=0, tiled=True)  6.5 us
    ppermute x7, waiting for transfers between devices, local(): lax.ppermute(parts[k], 'owner', [(i, i ^ k) for i in range(owners)])  4.35 us
    ppermute x3, starting transfers between devices, local(): lax.ppermute(shared, 'section', [(partner(i, k), i) for i in range(sectio...  3.55 us
    ppermute x3, waiting for transfers between devices, local(): lax.ppermute(shared, 'section', [(partner(i, k), i) for i in range(sectio...  3.46 us
  transfers between devices with their start and end apart: 11, of which 4 were waited for; matrix products, arithmetic and copies ran while one was open for 0% of the time, Pallas kernels for 16%

profile of v1, /device:TPU:0, one launch (start us, length us, event | category | flops | bytes accessed | tf_op | source)
XLA Modules:
  0.0 55.2 jit_solution(3158714353714930777)
XLA Ops:
  0.0 2.3 %shard_map.82 = (bf16[8,264,128]{2,1,0:T(8,128)(2,1)}, bf16[192,128]{1,0:T(8,128)(2,1)}) custom-call(s32[2,8]{1,0:T(2,128)} %bitcast.14, bf16[16,128,128]{2,1,0:T(8,128)(2,1)} %bitcast.11, s32[2,1024]{1,0:T(2,128)} %refs_5_.1, s32[2,1024]{1,0:T(2,128)} %refs_6_.1, s32[8,64]{1,0:T(8,128)} %bitcast.18, bf16[128,128]{1,0:T(8,128)(2,1)} %bitcast.17), custom_call_target="tpu_custom_call" | custom-call | tf_op jit(solution)/shard_map/pallas_call | solution.py:31
  2.4 0.0 copy-start
  2.4 6.5 %all-to-all-start = ((bf16[8,264,128]{2,1,0:T(8,128)(2,1)}), bf16[8,264,128]{2,1,0:T(8,128)(2,1)S(1)}, u32[]{:S(2)}, u32[]{:S(2)}) async-start(bf16[8,264,128]{2,1,0:T(8,128)(2,1)} %get-tuple-element.16), calls=%async_computation | async-start | bytes 1081344 | tf_op jit(solution)/shard_map/all_to_all | solution.py:364
  8.9 2.5 %collective-permute-start.2 = (bf16[192,128]{1,0:T(8,128)(2,1)S(1)}, bf16[192,128]{1,0:T(8,128)(2,1)S(1)}, u32[]{:S(2)}, u32[]{:S(2)}) collective-permute-start(bf16[192,128]{1,0:T(8,128)(2,1)S(1)} %copy-done.1), channel_id=1, source_target_pairs={{24,0},{16,8},{8,16},{0,24},{25,1},{17,9},{9,17},{1,25},{26,2},{18... | collective-permute-start | bytes 147464 | tf_op jit(solution)/shard_map/ppermute | solution.py:372
  11.4 0.5 collective-permute-start.1
  11.9 0.5 collective-permute-start
  12.4 0.1 stack.23.scalar_ref
  12.5 1.4 %collective-permute-done.2.refs_3_ = bf16[192,128]{1,0:T(8,128)(2,1)S(1)} collective-permute-done((bf16[192,128]{1,0:T(8,128)(2,1)S(1)}, bf16[192,128]{1,0:T(8,128)(2,1)S(1)}, u32[]{:S(2)}, u32[]{:S(2)}) %collective-permute-start.2) | collective-permute-done | bytes 49184 | tf_op jit(solution)/shard_map/ppermute | solution.py:372
  13.9 1.5 %collective-permute-done.1.refs_2_ = bf16[192,128]{1,0:T(8,128)(2,1)S(1)} collective-permute-done((bf16[192,128]{1,0:T(8,128)(2,1)S(1)}, bf16[192,128]{1,0:T(8,128)(2,1)S(1)}, u32[]{:S(2)}, u32[]{:S(2)}) %collective-permute-start.1) | collective-permute-done | bytes 49184 | tf_op jit(solution)/shard_map/ppermute | solution.py:372
  15.5 0.5 collective-permute-done.refs_1_
  16.0 1.6 %shard_map.83 = (bf16[4,128,128]{2,1,0:T(8,128)(2,1)S(1)}, bf16[264,128]{1,0:T(8,128)(2,1)S(1)}, bf16[264,128]{1,0:T(8,128)(2,1)S(1)}, bf16[264,128]{1,0:T(8,128...) custom-call(s32[6]{0:T(128)S(1)} %stack.23.scalar_ref, ...), custom_call_target="tpu_custom_call" | custom-call | tf_op jit(solution)/shard_map/pallas_call | solution.py:31
  17.7 0.0 collective-permute-start.3
  17.7 1.9 %collective-permute-start.4 = (bf16[264,128]{1,0:T(8,128)(2,1)S(1)}, bf16[264,128]{1,0:T(8,128)(2,1)S(1)}, u32[]{:S(2)}, u32[]{:S(2)}) collective-permute-start(bf16[264,128]{1,0:T(8,128)(2,1)S(1)} %get-tuple-element.21), channel_id=1, source_target_pairs={{0,2},{1,3},{2,0},{3,1},{4,6},{5,7},{6,4},{7,5},{8,10},{9,11},{10,... | collective-permute-start | bytes 202760 | tf_op jit(solution)/shard_map/ppermute | solution.py:401
  19.6 4.2 %shard_map.84.table_ref = f32[2048,128]{1,0:T(8,128)S(1)} custom-call(s32[32,128]{1,0:T(8,128)S(1)} %bitcast.16, bf16[4096,128]{1,0:T(8,128)(2,1)S(1)} %copy-done.5), custom_call_target="tpu_custom_call" | custom-call | flops 2147483648 | bytes 10502144 | tf_op jit(solution)/shard_map/pallas_call | solution.py:31
  23.8 0.2 collective-permute-start.5
  24.0 2.6 %collective-permute-start.6 = (bf16[264,128]{1,0:T(8,128)(2,1)}, bf16[264,128]{1,0:T(8,128)(2,1)S(1)}, u32[]{:S(2)}, u32[]{:S(2)}) collective-permute-start(bf16[264,128]{1,0:T(8,128)(2,1)} %get-tuple-element.23), channel_id=1, source_target_pairs={{0,4},{1,5},{2,6},{3,7},{4,0},{5,1},{6,2},{7,3},{8,12},{9,13},{10,... | collective-permute-start | bytes 202760 | tf_op jit(solution)/shard_map/ppermute | solution.py:401
  26.7 3.4 %collective-permute-start.8 = (bf16[264,128]{1,0:T(8,128)(2,1)S(1)}, bf16[264,128]{1,0:T(8,128)(2,1)S(1)}, u32[]{:S(2)}, u32[]{:S(2)}) collective-permute-start(bf16[264,128]{1,0:T(8,128)(2,1)S(1)} %get-tuple-element.25), channel_id=1, source_target_pairs={{0,6},{1,7},{2,4},{3,5},{4,2},{5,3},{6,0},{7,1},{8,14},{9,15},{10,... | collective-permute-start | bytes 202760 | tf_op jit(solution)/shard_map/ppermute | solution.py:401
  30.1 0.2 collective-permute-start.9
  30.3 0.0 all-to-all-done.first_ref
  30.3 2.7 %shard_map.85.joined_ref = bf16[8,256,128]{2,1,0:T(8,128)(2,1)S(1)} custom-call(bf16[8,264,128]{2,1,0:T(8,128)(2,1)S(1)} %all-to-all-done.first_ref, bf16[4,128,128]{2,1,0:T(8,128)(2,1)S(1)} %get-tuple-element.18.weights_ref, f32[2048,128]{1,0:T(8,128)S(1)} %shard_map.84.table_ref), custom_call_target="tpu_custom_call" | custom-call | flops 1073741824 | bytes 3325960 | tf_op jit(solution)/shard_map/pallas_call | solution.py:31
  33.1 4.3 %collective-permute-done.7.refs_5_ = bf16[264,128]{1,0:T(8,128)(2,1)S(1)} collective-permute-done((bf16[264,128]{1,0:T(8,128)(2,1)S(1)}, bf16[264,128]{1,0:T(8,128)(2,1)S(1)}, u32[]{:S(2)}, u32[]{:S(2)}) %collective-permute-start.7) | collective-permute-done | bytes 67616 | tf_op jit(solution)/shard_map/ppermute | solution.py:401
  37.4 3.9 %shard_map.86 = f32[128,128]{1,0:T(8,128)S(1)} custom-call(s32[6]{0:T(128)S(1)} %stack.23.scalar_ref, bf16[8,264,128]{2,1,0:T(8,128)(2,1)S(1)} %all-to-all-done.first_ref, bf16[8,256,128]{2,1,0:T(8,128)(2,1)S(1)} %shard_map.85.joined_ref, bf16[4,128,128]{2,1,0:T(8,128)(2,1)S(1)} %get-tuple-element.18.weights_ref, f32[2048,128]{1,0:T(8,128)S(1)} %shard_map.84.table_ref, ...), custom_call_target="tpu_custom_call" | custom-call | flops 134217728 | bytes 3932168 | tf_op jit(solution)/shard_map/pallas_call | solution.py:31
  41.4 13.2 %all_to_all.10 = f32[32,4,128]{2,1,0:T(4,128)S(1)} all-to-all(f32[32,4,128]{2,1,0:T(4,128)S(1)} %bitcast.13), channel_id=1, replica_groups=mesh['section'=4,'owner'=8] {'section','owner'}, dimensions={0} | all-to-all | bytes 131072 | tf_op jit(solution)/shard_map/all_to_all | solution.py:432
  54.6 0.6 %reduce_sum.9 = f32[4,128]{1,0:T(4,128)} reduce(f32[32,4,128]{2,1,0:T(4,128)S(1)} %all_to_all.10, f32[]{:T(128)} %constant.26.clone.1), dimensions={0}, to_apply=%region_0.0 | reduce | flops 15872 | bytes 67588 | tf_op jit(solution)/shard_map/reduce_sum | solution.py:433
  (20 shorter events, 0.0 us)
Async XLA Ops:
  0.0 19.6 %copy-start.5 = (bf16[4096,128]{1,0:T(8,128)(2,1)S(1)}, bf16[4096,128]{1,0:T(8,128)(2,1)}, u32[]{:S(2)}) copy-start(bf16[4096,128]{1,0:T(8,128)(2,1)} %values_ref.1) | copy-start | bytes 3145732
  2.4 6.5 %copy-start.1 = (bf16[192,128]{1,0:T(8,128)(2,1)S(1)}, bf16[192,128]{1,0:T(8,128)(2,1)}, u32[]{:S(2)}) copy-start(bf16[192,128]{1,0:T(8,128)(2,1)} %get-tuple-element.17.refs_0_) | copy-start | bytes 147460
  2.4 13.6 %copy-start = (bf16[2,1024,128]{2,1,0:T(8,128)(2,1)S(1)}, bf16[2,1024,128]{2,1,0:T(8,128)(2,1)}, u32[]{:S(2)}) copy-start(bf16[2,1024,128]{2,1,0:T(8,128)(2,1)} %param.8) | copy-start | bytes 1572868
  2.4 27.9 %all-to-all-start = ((bf16[8,264,128]{2,1,0:T(8,128)(2,1)}), bf16[8,264,128]{2,1,0:T(8,128)(2,1)S(1)}, u32[]{:S(2)}, u32[]{:S(2)}) async-start(bf16[8,264,128]{2,1,0:T(8,128)(2,1)} %get-tuple-element.16), calls=%async_computation | async-start | bytes 1081344 | tf_op jit(solution)/shard_map/all_to_all | solution.py:364
  8.9 5.1 %collective-permute-start.2 = (bf16[192,128]{1,0:T(8,128)(2,1)S(1)}, bf16[192,128]{1,0:T(8,128)(2,1)S(1)}, u32[]{:S(2)}, u32[]{:S(2)}) collective-permute-start(bf16[192,128]{1,0:T(8,128)(2,1)S(1)} %copy-done.1), channel_id=1, source_target_pairs={{24,0},{16,8},{8,16},{0,24},{25,1},{17,9},{9,17},{1,25},{26,2},{18... | collective-permute-start | bytes 147464 | tf_op jit(solution)/shard_map/ppermute | solution.py:372
  11.4 4.1 %collective-permute-start.1 = (bf16[192,128]{1,0:T(8,128)(2,1)S(1)}, bf16[192,128]{1,0:T(8,128)(2,1)S(1)}, u32[]{:S(2)}, u32[]{:S(2)}) collective-permute-start(bf16[192,128]{1,0:T(8,128)(2,1)S(1)} %copy-done.1), channel_id=1, source_target_pairs={{16,0},{24,8},{0,16},{8,24},{17,1},{25,9},{1,17},{9,25},{18,2},{26... | collective-permute-start | bytes 147464 | tf_op jit(solution)/shard_map/ppermute | solution.py:372
  11.9 4.1 %collective-permute-start = (bf16[192,128]{1,0:T(8,128)(2,1)S(1)}, bf16[192,128]{1,0:T(8,128)(2,1)S(1)}, u32[]{:S(2)}, u32[]{:S(2)}) collective-permute-start(bf16[192,128]{1,0:T(8,128)(2,1)S(1)} %copy-done.1), channel_id=1, source_target_pairs={{8,0},{0,8},{24,16},{16,24},{9,1},{1,9},{25,17},{17,25},{10,2},{2,... | collective-permute-start | bytes 147464 | tf_op jit(solution)/shard_map/ppermute | solution.py:372
  12.4 3.6 %copy-start.4 = (s32[2,8,1]{1,2,0:T(1,128)S(1)}, s32[2,8,1]{1,2,0:T(1,128)}, u32[]{:S(2)}) copy-start(s32[2,8,1]{1,2,0:T(1,128)} %param.11) | copy-start | bytes 196
  12.4 3.6 %copy-start.2 = (s32[2,1024]{1,0:T(2,128)S(1)}, s32[2,1024]{1,0:T(2,128)}, u32[]{:S(2)}) copy-start(s32[2,1024]{1,0:T(2,128)} %refs_5_.1) | copy-start | bytes 24580
  12.4 3.6 %copy-start.3 = (s32[2,1024]{1,0:T(2,128)S(1)}, s32[2,1024]{1,0:T(2,128)}, u32[]{:S(2)}) copy-start(s32[2,1024]{1,0:T(2,128)} %refs_6_.1) | copy-start | bytes 24580
  12.5 7.1 %copy-start.6 = (s32[4096]{0:T(1024)S(1)}, s32[4096]{0:T(1024)}, u32[]{:S(2)}) copy-start(s32[4096]{0:T(1024)} %param.14) | copy-start | bytes 49156
  17.7 9.0 %collective-permute-start.3 = (bf16[264,128]{1,0:T(8,128)(2,1)S(1)}, bf16[264,128]{1,0:T(8,128)(2,1)S(1)}, u32[]{:S(2)}, u32[]{:S(2)}) collective-permute-start(bf16[264,128]{1,0:T(8,128)(2,1)S(1)} %get-tuple-element.20), channel_id=1, source_target_pairs={{0,1},{1,0},{2,3},{3,2},{4,5},{5,4},{6,7},{7,6},{8,9},{9,8},{10,11... | collective-permute-start | bytes 202760 | tf_op jit(solution)/shard_map/ppermute | solution.py:401
  17.7 12.5 %collective-permute-start.4 = (bf16[264,128]{1,0:T(8,128)(2,1)S(1)}, bf16[264,128]{1,0:T(8,128)(2,1)S(1)}, u32[]{:S(2)}, u32[]{:S(2)}) collective-permute-start(bf16[264,128]{1,0:T(8,128)(2,1)S(1)} %get-tuple-element.21), channel_id=1, source_target_pairs={{0,2},{1,3},{2,0},{3,1},{4,6},{5,7},{6,4},{7,5},{8,10},{9,11},{10,... | collective-permute-start | bytes 202760 | tf_op jit(solution)/shard_map/ppermute | solution.py:401
  23.8 9.2 %collective-permute-start.5 = (bf16[264,128]{1,0:T(8,128)(2,1)}, bf16[264,128]{1,0:T(8,128)(2,1)S(1)}, u32[]{:S(2)}, u32[]{:S(2)}) collective-permute-start(bf16[264,128]{1,0:T(8,128)(2,1)} %get-tuple-element.22), channel_id=1, source_target_pairs={{0,3},{1,2},{2,1},{3,0},{4,7},{5,6},{6,5},{7,4},{8,11},{9,10},{10,... | collective-permute-start | bytes 202760 | tf_op jit(solution)/shard_map/ppermute | solution.py:401
  24.0 9.0 %collective-permute-start.6 = (bf16[264,128]{1,0:T(8,128)(2,1)}, bf16[264,128]{1,0:T(8,128)(2,1)S(1)}, u32[]{:S(2)}, u32[]{:S(2)}) collective-permute-start(bf16[264,128]{1,0:T(8,128)(2,1)} %get-tuple-element.23), channel_id=1, source_target_pairs={{0,4},{1,5},{2,6},{3,7},{4,0},{5,1},{6,2},{7,3},{8,12},{9,13},{10,... | collective-permute-start | bytes 202760 | tf_op jit(solution)/shard_map/ppermute | solution.py:401
  26.7 10.7 %collective-permute-start.7 = (bf16[264,128]{1,0:T(8,128)(2,1)S(1)}, bf16[264,128]{1,0:T(8,128)(2,1)S(1)}, u32[]{:S(2)}, u32[]{:S(2)}) collective-permute-start(bf16[264,128]{1,0:T(8,128)(2,1)S(1)} %get-tuple-element.24), channel_id=1, source_target_pairs={{0,5},{1,4},{2,7},{3,6},{4,1},{5,0},{6,3},{7,2},{8,13},{9,12},{10,... | collective-permute-start | bytes 202760 | tf_op jit(solution)/shard_map/ppermute | solution.py:401
  26.7 10.7 %collective-permute-start.8 = (bf16[264,128]{1,0:T(8,128)(2,1)S(1)}, bf16[264,128]{1,0:T(8,128)(2,1)S(1)}, u32[]{:S(2)}, u32[]{:S(2)}) collective-permute-start(bf16[264,128]{1,0:T(8,128)(2,1)S(1)} %get-tuple-element.25), channel_id=1, source_target_pairs={{0,6},{1,7},{2,4},{3,5},{4,2},{5,3},{6,0},{7,1},{8,14},{9,15},{10,... | collective-permute-start | bytes 202760 | tf_op jit(solution)/shard_map/ppermute | solution.py:401
  30.1 7.3 %collective-permute-start.9 = (bf16[264,128]{1,0:T(8,128)(2,1)S(1)}, bf16[264,128]{1,0:T(8,128)(2,1)S(1)}, u32[]{:S(2)}, u32[]{:S(2)}) collective-permute-start(bf16[264,128]{1,0:T(8,128)(2,1)S(1)} %get-tuple-element.26), channel_id=1, source_target_pairs={{0,7},{1,6},{2,5},{3,4},{4,3},{5,2},{6,1},{7,0},{8,15},{9,14},{10,... | collective-permute-start | bytes 202760 | tf_op jit(solution)/shard_map/ppermute | solution.py:401

commit v2 on v1

v2 whole, which is shorter than its diff:
```python
import functools
import math

import jax
import jax.numpy as jnp
from jax import lax
from jax.experimental import pallas as pl
from jax.experimental.pallas import tpu as pltpu
from jax.sharding import PartitionSpec as P


CAP = 2
KEYS_OWN = 2048
GRP_DEV = 4
FIELDS = 3
BF16 = jnp.bfloat16
F32 = jnp.float32
I32 = jnp.int32


def run(kernel, ins, outs, scratch=(), scalars=(), flops=0, away=False):
    several = isinstance(outs, list)
    shapes = [jax.ShapeDtypeStruct(shape, dtype) for shape, dtype in (outs if several else [outs])]
    held = shapes + [x for k, x in enumerate(ins) if k not in scalars and not away]
    size = sum(math.prod(x.shape) * x.dtype.itemsize for x in held)
    for entry in scratch:
        size += 2 * math.prod(getattr(entry, "shape", ())) * 4
    place = pl.BlockSpec(memory_space=pltpu.VMEM)
    spaces = [pltpu.SMEM if k in scalars else pltpu.HBM if away else pltpu.VMEM for k in range(len(ins))]
    return pl.pallas_call(
        kernel,
        out_shape=shapes if several else shapes[0],
        in_specs=[pl.BlockSpec(memory_space=space) for space in spaces],
        out_specs=[place] * len(shapes) if several else place,
        scratch_shapes=list(scratch),
        compiler_params=pltpu.CompilerParams(vmem_limit_bytes=60 * 2**20 if away else min(size + 4 * 2**20, 60 * 2**20)),
        cost_estimate=pl.CostEstimate(flops=flops, bytes_accessed=size, transcendentals=0) if flops else None,
    )(*ins)


def walk_blocks(dest_ref, count_ref, owners, visit):
    batches, blocks = dest_ref.shape

    def clear(owner, carry):
        count_ref[owner] = 0
        return carry

    lax.fori_loop(0, owners, clear, 0)
    for micro in range(batches):

        def step(block, carry, micro=micro):
            owner = dest_ref[micro, block]
            slot = count_ref[owner]
            count_ref[owner] = slot + 1
            visit(micro, block, owner, slot)
            return carry

        lax.fori_loop(0, blocks, step, 0, unroll=min(blocks, 8))


def put_block(slots, source, owner_at, slot, out_ref, meta_ref):
    values, keys, groups = source
    rows = values.shape[0]
    out_ref[owner_at, pl.ds(pl.multiple_of(slot * rows, rows), rows), :] = values
    high = ((groups >> 7) * (KEYS_OWN // 128) + (keys >> 7)).astype(F32)
    low = (groups & 127).astype(F32)
    for field, part in enumerate((high, (keys & 127).astype(F32), low)):
        meta_ref[owner_at, pl.ds(field * slots + slot, 1), :] = part


def key_of(high, low):
    return (high.astype(I32) & (KEYS_OWN // 128 - 1)) * 128 + low.astype(I32)


def group_of(high, low):
    return (high.astype(I32) // (KEYS_OWN // 128) * 128).astype(F32) + low


def share_bits(words_ref, weight_ref, shared_ref):
    columns = weight_ref.shape[0]
    shared_ref[:columns, :] = weight_ref[...]
    words = words_ref[...]
    micros, length = words.shape
    parts = jnp.concatenate([words & 255, words >> 8], axis=0).astype(F32).astype(BF16)
    width = min(length, 128)
    spread = lax.broadcasted_iota(I32, (width, width * 16), 1) // 16 == lax.broadcasted_iota(I32, (width, width * 16), 0)
    spread = jnp.where(spread, 1.0, 0.0).astype(BF16)
    place = lax.broadcasted_iota(I32, (micros, width * 16), 1) & 15
    for turn in range(length // width):
        found = jnp.dot(parts[:, turn * width : (turn + 1) * width], spread, preferred_element_type=F32).astype(I32)
        bits = (jnp.where(place < 8, found[:micros], found[micros:]) >> (place & 7)) & 1
        stacked = jnp.concatenate([bits[:, k : k + 128] for k in range(0, width * 16, 128)], axis=0)
        start = columns + turn * stacked.shape[0]
        shared_ref[start : start + stacked.shape[0], :] = stacked.astype(F32).astype(BF16)


def pack_first(few, slots, me_ref, *refs):
    sources, shared_ref, outs, held = refs[:6], refs[6], refs[7:-10], refs[-10:-4]
    buffer_ref, meta_ref, count_ref, sems = refs[-4:]
    dest_ref, values_ref, keys_ref, groups_ref, words_ref, weight_ref = held
    owners = buffer_ref.shape[0]
    blocks = dest_ref.shape[1]
    rows = values_ref.shape[1]
    copies = [pltpu.make_async_copy(source, target, sems.at[k]) for k, (source, target) in enumerate(zip(sources, held))]
    for copy in copies:
        copy.start()
    meta_ref[...] = jnp.zeros_like(meta_ref)
    buffer_ref[...] = jnp.zeros_like(buffer_ref)
    me = me_ref[0]
    copies[4].wait()
    copies[5].wait()
    share_bits(words_ref, weight_ref, shared_ref)
    for copy in copies[:4]:
        copy.wait()

    def visit(micro, block, owner, slot):
        lanes = pl.ds(pl.multiple_of(block * rows, rows), rows)
        source = (values_ref[micro * blocks + block], keys_ref[pl.ds(micro, 1), lanes], groups_ref[pl.ds(micro, 1), lanes])
        put_block(slots, source, owner ^ me if few else owner, slot, buffer_ref, meta_ref)

    walk_blocks(dest_ref, count_ref, owners, visit)
    buffer_ref[:, slots * rows :, :] = meta_ref[...].astype(BF16)
    if few:
        for k, out in enumerate(outs):
            out[...] = buffer_ref[k]
    else:
        outs[0][...] = buffer_ref[...]


def build_table(keys_ref, values_ref, out_ref, wide_ref):
    chunks, lanes = keys_ref.shape
    columns = values_ref.shape[1]
    tiles = out_ref.shape[0] // lanes // 2
    sub = lax.broadcasted_iota(I32, (lanes, lanes), 0)
    keys = keys_ref[...]
    upper = jnp.where(keys >= tiles * lanes, 1.0, 0.0).T
    middle = (keys >> 7) & (tiles - 1)
    low = []
    for chunk in range(chunks):
        low.append(jnp.where(sub == (keys[chunk : chunk + 1] & (lanes - 1)), 1.0, 0.0).astype(BF16))
        flag = jnp.broadcast_to(upper[:, chunk : chunk + 1], (lanes, columns)).astype(BF16)
        part = values_ref[chunk * lanes : (chunk + 1) * lanes, :]
        high_part = part * flag
        wide_ref[chunk * lanes : (chunk + 1) * lanes, :columns] = part - high_part
        wide_ref[chunk * lanes : (chunk + 1) * lanes, columns:] = high_part

    def tile_step(tile, carry):
        here = jnp.where(middle == tile, 1.0, 0.0)
        hot = [low[chunk] * jnp.broadcast_to(here[chunk : chunk + 1], (lanes, lanes)).astype(BF16) for chunk in range(chunks)]
        total = jnp.dot(jnp.concatenate(hot, axis=1), wide_ref[...], preferred_element_type=F32)
        out_ref[pl.ds(pl.multiple_of(tile * lanes, lanes), lanes), :] = total[:, :columns]
        out_ref[pl.ds(pl.multiple_of((tiles + tile) * lanes, lanes), lanes), :] = total[:, columns:]
        return carry

    lax.fori_loop(0, tiles, tile_step, 0)


def place_bits(sections, scalar_ref, *refs):
    shared, (dest_ref, weights_ref, out_ref, kept_ref, count_ref) = refs[:sections], refs[sections:]
    owners = out_ref.shape[0]
    batches, blocks = dest_ref.shape
    columns = weights_ref.shape[1]
    home = scalar_ref[sections + 1]
    kept = shared[0][columns:, :].astype(F32)
    for ref in shared[1:]:
        kept = kept * ref[columns:, :].astype(F32)
    kept_ref[...] = kept
    micros = kept.shape[0] // blocks
    for k, ref in enumerate(shared):
        weights_ref[scalar_ref[k]] = (ref[:columns, :].astype(F32) * 0.5).astype(BF16)
    out_ref[...] = jnp.zeros_like(out_ref)

    def visit(micro, block, owner, slot):
        out_ref[owner, pl.ds(slot, 1), :] = kept_ref[pl.ds(block * micros + home * batches + micro, 1), :]

    walk_blocks(dest_ref, count_ref, owners, visit)


def chain(values, weights):
    for weight in weights:
        half = jnp.dot(values, weight, preferred_element_type=F32)
        values = (values.astype(F32) + (half + half * jnp.tanh(half))).astype(BF16)
    return values


def join_rows(values, weights, rows, place_of, table_ref, found_ref):
    count = values.shape[0] // rows
    for block in range(count):
        for row in range(rows):
            found_ref[block * rows + row : block * rows + row + 1, :] = table_ref[pl.ds(place_of(block, row), 1), :]
    return (chain(values, weights).astype(F32) * found_ref[...]).astype(BF16)


def start_keys(parts, slots, span, keys_ref, places_ref, sem):
    for k, part in enumerate(parts):
        meta = part[span:, :].astype(F32)
        keys_ref[k] = key_of(meta[:slots], meta[slots : 2 * slots])
    copy = pltpu.make_async_copy(keys_ref, places_ref, sem)
    copy.start()
    return copy


def join_parts(parts, first, slots, span, weights, table_ref, found_ref, places_ref):
    values = jnp.concatenate([part[:span, :] for part in parts], axis=0)
    return join_rows(
        values,
        weights,
        span // slots,
        lambda block, row: places_ref[first + block // slots, block % slots, row],
        table_ref,
        found_ref,
    )


def sums_of(parts, kepts, joined, slots, span, groups):
    sub = lax.broadcasted_iota(I32, (groups, span // slots), 0).astype(F32)
    hot = []
    for part, kept in zip(parts, kepts):
        meta = part[span:, :].astype(F32)
        keys = group_of(meta[:slots], meta[2 * slots : 3 * slots])
        keys = jnp.where(kept[:slots] > 0.5, keys, -1.0)
        hot += [jnp.where(sub == keys[j : j + 1], 1.0, 0.0).astype(BF16) for j in range(slots)]
    return jnp.dot(jnp.concatenate(hot, axis=1), joined, preferred_element_type=F32)


def join_only(slots, weights_ref, table_ref, *refs):
    parts, (out_ref, keys_ref, found_ref, places_ref, sem) = refs[:-5], refs[-5:]
    span = out_ref.shape[1]
    group = found_ref.shape[0] // span
    copy = start_keys(parts, slots, span, keys_ref, places_ref, sem)
    weights = [weights_ref[j] for j in range(weights_ref.shape[0])]
    copy.wait()
    for at in range(0, len(parts), group):
        joined = join_parts(parts[at : at + group], at, slots, span, weights, table_ref, found_ref, places_ref)
        out_ref[at : at + group] = joined.reshape(group, span, joined.shape[1])


def join_sum(slots, span, new, old, carried, scalar_ref, kept_ref, weights_ref, table_ref, *refs):
    news, olds, refs = refs[: len(new)], refs[len(new) : len(new) + len(old)], refs[len(new) + len(old) :]
    before, (out_ref, keys_ref, found_ref, places_ref, sem) = refs[:-5], refs[-5:]
    groups = out_ref.shape[0]
    group = found_ref.shape[0] // span
    me = scalar_ref[weights_ref.shape[0]]
    copy = start_keys(news, slots, span, keys_ref, places_ref, sem)
    weights = [weights_ref[j] for j in range(weights_ref.shape[0])]
    total = before[-1][...] if carried else jnp.zeros(out_ref.shape, F32)
    if old:
        joined = before[0][...].reshape(len(old) * span, out_ref.shape[1])
        total += sums_of(olds, [kept_ref[me ^ k] for k in old], joined, slots, span, groups)
    copy.wait()
    for at in range(0, len(new), group):
        these = news[at : at + group]
        joined = join_parts(these, at, slots, span, weights, table_ref, found_ref, places_ref)
        total += sums_of(these, [kept_ref[me ^ k] for k in new[at : at + group]], joined, slots, span, groups)
    out_ref[...] = total


def join_all(slots, span, kept_ref, weights_ref, table_ref, first_ref, out_ref, keys_ref, found_ref, places_ref, sem):
    groups = out_ref.shape[0]
    meta = first_ref[:, span:, :].astype(F32)
    keys_ref[...] = key_of(meta[:, :slots], meta[:, slots : 2 * slots])
    copy = pltpu.make_async_copy(keys_ref, places_ref, sem)
    copy.start()
    weights = [weights_ref[j] for j in range(weights_ref.shape[0])]
    out_ref[...] = jnp.zeros_like(out_ref)
    copy.wait()

    def step(source, carry):
        part = first_ref.at[source]
        joined = join_parts([part], source, slots, span, weights, table_ref, found_ref, places_ref)
        out_ref[...] += sums_of([part], [kept_ref[source]], joined, slots, span, groups)
        return carry

    lax.fori_loop(0, first_ref.shape[0], step, 0)


def few_owners(owners):
    return 4 < owners <= 8 and owners & (owners - 1) == 0


def far_first(owners):
    return sorted(range(1, owners), key=lambda k: -(k // 2) * owners + k)


def local(
    probe_values,
    probe_keys,
    group_ids,
    block_dest,
    filter_bits,
    section_weights,
    build_keys,
    build_values,
):
    sections = lax.axis_size("section")
    owners = lax.axis_size("owner")
    home = lax.axis_index("section").astype(I32)
    batches, block_count = block_dest.shape[:2]
    columns = probe_values.shape[2]
    rows = probe_values.shape[1] // block_count
    groups_all = GRP_DEV * sections * owners
    slots = batches * CAP
    span = slots * rows
    height = span + -(-FIELDS * slots // 8) * 8
    few = few_owners(owners)
    paired = sections & (sections - 1) == 0

    def partner(index, k):
        return index ^ k if paired else (index - k) % sections

    me = lax.axis_index("owner").astype(I32)
    scalars = jnp.stack([lax.rem(partner(home, k) - home + sections, sections) for k in range(sections)] + [me, home])
    dest = block_dest.reshape(batches, block_count)
    blocks = probe_values.reshape(batches * block_count, rows, columns)
    words = filter_bits[0]
    micros = words.shape[0]
    counts = pltpu.SMEM((owners,), I32)
    sources = [dest, blocks, probe_keys, group_ids, words, section_weights[0]]
    shared, *packed = run(
        functools.partial(pack_first, few, slots),
        [me.reshape(1)] + sources,
        [((columns + micros * block_count, columns), BF16)]
        + ([((height, columns), BF16)] * owners if few else [((owners, height, columns), BF16)]),
        [pltpu.SMEM(dest.shape, I32)]
        + [pltpu.VMEM(source.shape, source.dtype) for source in sources[1:]]
        + [
            pltpu.VMEM((owners, height, columns), BF16),
            pltpu.VMEM((owners, height - span, columns), F32),
            counts,
            pltpu.SemaphoreType.DMA((len(sources),)),
        ],
        scalars=(0,),
        away=True,
    )
    if few:
        for k in far_first(owners):
            packed[k] = lax.ppermute(packed[k], "owner", [(i, i ^ k) for i in range(owners)])
    else:
        packed = [lax.all_to_all(packed[0], "owner", split_axis=0, concat_axis=0, tiled=True)]

    received = [shared]
    for k in range(1, sections):
        received.append(lax.ppermute(shared, "section", [(partner(i, k), i) for i in range(sections)]))
    table = run(
        build_table,
        [build_keys.reshape(-1, 128), build_values],
        ((KEYS_OWN, columns), F32),
        [pltpu.VMEM((build_values.shape[0], 2 * columns), BF16)],
        flops=2 * KEYS_OWN * build_keys.shape[0] * columns,
    )
    weights, kept = run(
        functools.partial(place_bits, sections),
        [scalars] + received + [dest],
        [((sections, columns, columns), BF16), ((owners, 8, rows), F32)],
        [pltpu.VMEM((micros * block_count, rows), F32), counts],
        scalars=(0, 1 + sections),
    )
    kept = lax.all_to_all(kept, "owner", split_axis=0, concat_axis=0, tiled=True)

    def scratch(count, group):
        return [
            pltpu.VMEM((count, slots, rows), I32),
            pltpu.VMEM((group * span, columns), F32),
            pltpu.SMEM((count, slots, rows), I32),
            pltpu.SemaphoreType.DMA,
        ]

    work = 2 * KEYS_OWN * span * columns
    sums_shape = ((groups_all, columns), F32)
    if few:
        order = far_first(owners)
        near = [0, order[-1]]
        soon, middle, final = near + order[: owners // 4], order[owners // 2 : -1], order[owners // 4 : owners // 2]
        joined = run(
            functools.partial(join_only, slots),
            [weights, table] + [packed[k] for k in soon],
            ((len(soon), span, columns), BF16),
            scratch(len(soon), 2),
            flops=len(soon) * work,
        )
        sums = run(
            functools.partial(join_sum, slots, span, middle, soon, False),
            [scalars, kept, weights, table] + [packed[k] for k in middle + soon] + [joined],
            sums_shape,
            scratch(len(middle), 2),
            scalars=(0,),
            flops=len(middle) * work,
        )
        sums = run(
            functools.partial(join_sum, slots, span, final, [], True),
            [scalars, kept, weights, table] + [packed[k] for k in final] + [sums],
            sums_shape,
            scratch(len(final), 2),
            scalars=(0,),
            flops=len(final) * work,
        )
    else:
        sums = run(
            functools.partial(join_all, slots, span),
            [kept, weights, table, packed[0]],
            sums_shape,
            scratch(owners, 1),
            flops=owners * work,
        )
    parts = sums.reshape(sections * owners, GRP_DEV, columns)
    parts = lax.all_to_all(parts, ("section", "owner"), split_axis=0, concat_axis=0, tiled=True)
    return jnp.sum(parts, axis=0)


def solution(mesh):
    placed = (
        P("section", "owner", None),
        P("section", "owner"),
        P("section", "owner"),
        P("section", "owner", None),
        P("section", None, "owner"),
        P("section", None, None),
        P("owner"),
        P("owner", None),
    )
    return jax.shard_map(
        local, mesh=mesh, in_specs=placed, out_specs=P(("section", "owner"), None), check_vma=False
    )
```

time: 55.5 us -> 57.4 us (1.034)
  local copies, waits for them, and re-layouts: 0.11 us -> 1.98 us
  blocking collectives: 13.2 us -> 11.5 us
  waiting for transfers between devices: 7.82 us -> 8.87 us
  Pallas kernels: 14.9 us -> 15.8 us
    ppermute x7, waiting for transfers between devices: 4.35 us -> 7.2 us  [local(): lax.ppermute(packed[k], 'owner', [(i, i ^ k) for i in range(owners)])]
    ppermute x3, waiting for transfers between devices: 3.46 us -> 1.52 us  [local(): lax.ppermute(shared, 'section', [(partner(i, k), i) for i in range(sectio...]
    unnamed x14, local copies, waits for them, and re-layouts: 0.03 us -> 1.89 us
    all_to_all x1, blocking collectives: 13.2 us -> 11.5 us  [local(): lax.all_to_all(parts, ('section', 'owner'), split_axis=0, concat_axis=0,...]
    all_to_all x1, starting transfers between devices: 6.5 us -> 4.81 us  [local(): lax.all_to_all(kept, 'owner', split_axis=0, concat_axis=0, tiled=True)]
    ppermute x3, starting transfers between devices: 3.55 us -> 4.63 us  [local(): lax.ppermute(shared, 'section', [(partner(i, k), i) for i in range(sectio...]
    pallas_call x5 -> x6, Pallas kernels: 14.9 us -> 15.8 us  [run(): pl.pallas_call(kernel, out_shape=shapes if several else shapes[0], in_spe...]
  transfers between devices with their start and end apart: 11 -> 11, of which waited for: 4 -> 4; matrix products, arithmetic and copies ran while one was open for 0% -> 0% of each run, Pallas kernels for 16% -> 19%
where the time goes in v2:
time: 57.4 us; the launch traced here: 57.2 us
  starting transfers between devices  18.2 us (32%)
  Pallas kernels  15.8 us (28%)
  blocking collectives  11.5 us (20%)
  waiting for transfers between devices  8.87 us (15%)
  local copies, waits for them, and re-layouts  1.98 us (3%)
  other arithmetic  0.62 us (1%)
    pallas_call x6, Pallas kernels, run(): pl.pallas_call(kernel, out_shape=shapes if several else shapes[0], in_spe...  15.8 us
    all_to_all x1, blocking collectives, local(): lax.all_to_all(parts, ('section', 'owner'), split_axis=0, concat_axis=0,...  11.5 us
    ppermute x7, starting transfers between devices, local(): lax.ppermute(packed[k], 'owner', [(i, i ^ k) for i in range(owners)])  8.73 us
    ppermute x7, waiting for transfers between devices, local(): lax.ppermute(packed[k], 'owner', [(i, i ^ k) for i in range(owners)])  7.2 us
    all_to_all x1, starting transfers between devices, local(): lax.all_to_all(kept, 'owner', split_axis=0, concat_axis=0, tiled=True)  4.81 us
    ppermute x3, starting transfers between devices, local(): lax.ppermute(shared, 'section', [(partner(i, k), i) for i in range(sectio...  4.63 us
    unnamed x14, local copies, waits for them, and re-layouts  1.89 us
    ppermute x3, waiting for transfers between devices, local(): lax.ppermute(shared, 'section', [(partner(i, k), i) for i in range(sectio...  1.52 us
  transfers between devices with their start and end apart: 11, of which 4 were waited for; matrix products, arithmetic and copies ran while one was open for 0% of the time, Pallas kernels for 19%

profile of v2, /device:TPU:0, one launch (start us, length us, event | category | flops | bytes accessed | tf_op | source)
XLA Modules:
  0.0 57.2 jit_solution(14700201961298520662)
XLA Ops:
  0.0 2.3 %shard_map.82 = (bf16[192,128]{1,0:T(8,128)(2,1)}, bf16[528,128]{1,0:T(8,128)(2,1)}, bf16[528,128]{1,0:T(8,128)(2,1)}, bf16[528,128]{1,0:T(8,128)(2,1)}, bf16[52...) custom-call(s32[1]{0:T(128)} %bitcast.3.me_ref, ...), custom_call_target="tpu_custom_call" | custom-call | tf_op jit(solution)/shard_map/pallas_call | solution.py:30
  2.4 4.0 %collective-permute-start.2 = (bf16[192,128]{1,0:T(8,128)(2,1)}, bf16[192,128]{1,0:T(8,128)(2,1)S(1)}, u32[]{:S(2)}, u32[]{:S(2)}) collective-permute-start(bf16[192,128]{1,0:T(8,128)(2,1)} %get-tuple-element.16.refs_0_), channel_id=1, source_target_pairs={{24,0},{16,8},{8,16},{0,24},{25,1},{17,9},{9,17},{1,25},{26,2},{18... | collective-permute-start | bytes 147464 | tf_op jit(solution)/shard_map/ppermute | solution.py:343
  6.3 0.5 collective-permute-start.1
  6.8 0.1 collective-permute-start
  7.0 2.0 %collective-permute-start.5 = (bf16[528,128]{1,0:T(8,128)(2,1)}, bf16[528,128]{1,0:T(8,128)(2,1)S(1)}, u32[]{:S(2)}, u32[]{:S(2)}) collective-permute-start(bf16[528,128]{1,0:T(8,128)(2,1)} %get-tuple-element.21), channel_id=1, source_target_pairs={{0,2},{1,3},{2,0},{3,1},{4,6},{5,7},{6,4},{7,5},{8,10},{9,11},{10,... | collective-permute-start | bytes 405512 | tf_op jit(solution)/shard_map/ppermute | solution.py:337
  9.0 0.2 collective-permute-start.7
  9.1 1.5 %collective-permute-done.1.refs_2_ = bf16[192,128]{1,0:T(8,128)(2,1)S(1)} collective-permute-done((bf16[192,128]{1,0:T(8,128)(2,1)}, bf16[192,128]{1,0:T(8,128)(2,1)S(1)}, u32[]{:S(2)}, u32[]{:S(2)}) %collective-permute-start.1) | collective-permute-done | bytes 49184 | tf_op jit(solution)/shard_map/ppermute | solution.py:343
  10.6 3.6 %collective-permute-start.8 = (bf16[528,128]{1,0:T(8,128)(2,1)}, bf16[528,128]{1,0:T(8,128)(2,1)S(1)}, u32[]{:S(2)}, u32[]{:S(2)}) collective-permute-start(bf16[528,128]{1,0:T(8,128)(2,1)} %get-tuple-element.25), channel_id=1, source_target_pairs={{0,6},{1,7},{2,4},{3,5},{4,2},{5,3},{6,0},{7,1},{8,14},{9,15},{10,... | collective-permute-start | bytes 405512 | tf_op jit(solution)/shard_map/ppermute | solution.py:337
  14.3 0.0 copy-start.3
  14.3 1.2 %copy-done.3 = bf16[4096,128]{1,0:T(8,128)(2,1)S(1)} copy-done((bf16[4096,128]{1,0:T(8,128)(2,1)S(1)}, bf16[4096,128]{1,0:T(8,128)(2,1)}, u32[]{:S(2)}) %copy-start.3) | copy-done | bytes 1048600
  15.5 4.2 %shard_map.84.table_ref = f32[2048,128]{1,0:T(8,128)S(1)} custom-call(s32[32,128]{1,0:T(8,128)S(1)} %bitcast.14, bf16[4096,128]{1,0:T(8,128)(2,1)S(1)} %copy-done.3), custom_call_target="tpu_custom_call" | custom-call | flops 2147483648 | bytes 10502144 | tf_op jit(solution)/shard_map/pallas_call | solution.py:30
  19.8 0.1 stack.23.scalar_ref
  19.9 0.7 %copy-done.1 = bf16[192,128]{1,0:T(8,128)(2,1)S(1)} copy-done((bf16[192,128]{1,0:T(8,128)(2,1)S(1)}, bf16[192,128]{1,0:T(8,128)(2,1)}, u32[]{:S(2)}) %copy-start.1) | copy-done | bytes 49176
  20.5 1.3 %shard_map.83 = (bf16[4,128,128]{2,1,0:T(8,128)(2,1)S(1)}, f32[8,8,128]{2,1,0:T(8,128)}) custom-call(s32[6]{0:T(128)S(1)} %stack.23.scalar_ref, bf16[192,128]{1,0:T(8,128)(2,1)S(1)} %copy-done.1, bf16[192,128]{1,0:T(8,128)(2,1)S(1)} %collective-permute-done.refs_1_, bf16[192,128]{1,0:T(8,128)(2,1)S(1)} %collective-permute-done.1.refs_2_, ...), custom_call_target="tpu_custom_call" | custom-call | tf_op jit(solution)/shard_map/pallas_call | solution.py:30
  21.8 4.8 %all-to-all-start = ((f32[8,8,128]{2,1,0:T(8,128)}), f32[8,8,128]{2,1,0:T(8,128)S(1)}, u32[]{:S(2)}, u32[]{:S(2)}) async-start(f32[8,8,128]{2,1,0:T(8,128)} %get-tuple-element.17), calls=%async_computation | async-start | bytes 65536 | tf_op jit(solution)/shard_map/all_to_all | solution.py:358
  26.7 3.0 %collective-permute-start.3 = (bf16[528,128]{1,0:T(8,128)(2,1)S(1)}, bf16[528,128]{1,0:T(8,128)(2,1)S(1)}, u32[]{:S(2)}, u32[]{:S(2)}) collective-permute-start(bf16[528,128]{1,0:T(8,128)(2,1)S(1)} %copy-done.6), channel_id=1, source_target_pairs={{0,4},{1,5},{2,6},{3,7},{4,0},{5,1},{6,2},{7,3},{8,12},{9,13},{10,... | collective-permute-start | bytes 405512 | tf_op jit(solution)/shard_map/ppermute | solution.py:337
  29.7 2.7 %shard_map.85.refs_6_ = bf16[4,512,128]{2,1,0:T(8,128)(2,1)S(1)} custom-call(bf16[4,128,128]{2,1,0:T(8,128)(2,1)S(1)} %get-tuple-element.18.weights_ref, f32[2048,128]{1,0:T(8,128)S(1)} %shard_map.84.table_ref, bf16[528,128]{1,0:T(8,128)(2,1)S(1)} %copy-done, bf16[528,128]{1,0:T(8,128)(2,1)S(1)} %collective-permute-done.7.refs_1_.refs_3_, ...), custom_call_target="tpu_custom_call" | custom-call | flops 1073741824 | bytes 3325960 | tf_op jit(solution)/shard_map/pallas_call | solution.py:30
  32.4 0.2 all-to-all-done.kept_ref
  32.6 2.7 %shard_map.86.refs_2_ = f32[128,128]{1,0:T(8,128)S(1)} custom-call(s32[6]{0:T(128)S(1)} %stack.23.scalar_ref, f32[8,8,128]{2,1,0:T(8,128)S(1)} %all-to-all-done.kept_ref, bf16[4,128,128]{2,1,0:T(8,128)(2,1)S(1)} %get-tuple-element.18.weights_ref, f32[2048,128]{1,0:T(8,128)S(1)} %shard_map.84.table_ref, bf16[528,128]{1,0:T(8,128)(2,1)S(1)} %collective-permute-done.5.refs_0_, ...), custom_call_target="tpu_custom_call" | custom-call | flops 536870912 | bytes 3678216 | tf_op jit(solution)/shard_map/pallas_call | solution.py:30
  35.3 5.4 %collective-permute-done.3.refs_0_ = bf16[528,128]{1,0:T(8,128)(2,1)S(1)} collective-permute-done((bf16[528,128]{1,0:T(8,128)(2,1)S(1)}, bf16[528,128]{1,0:T(8,128)(2,1)S(1)}, u32[]{:S(2)}, u32[]{:S(2)}) %collective-permute-start.3) | collective-permute-done | bytes 135200 | tf_op jit(solution)/shard_map/ppermute | solution.py:337
  40.7 1.8 %collective-permute-done.4.refs_1_ = bf16[528,128]{1,0:T(8,128)(2,1)S(1)} collective-permute-done((bf16[528,128]{1,0:T(8,128)(2,1)S(1)}, bf16[528,128]{1,0:T(8,128)(2,1)S(1)}, u32[]{:S(2)}, u32[]{:S(2)}) %collective-permute-start.4) | collective-permute-done | bytes 135200 | tf_op jit(solution)/shard_map/ppermute | solution.py:337
  42.5 2.5 %shard_map.87 = f32[128,128]{1,0:T(8,128)S(1)} custom-call(s32[6]{0:T(128)S(1)} %stack.23.scalar_ref, f32[8,8,128]{2,1,0:T(8,128)S(1)} %all-to-all-done.kept_ref, bf16[4,128,128]{2,1,0:T(8,128)(2,1)S(1)} %get-tuple-element.18.weights_ref, f32[2048,128]{1,0:T(8,128)S(1)} %shard_map.84.table_ref, bf16[528,128]{1,0:T(8,128)(2,1)S(1)} %collective-permute-done.3.refs_0_, ...), custom_call_target="tpu_custom_call" | custom-call | flops 536870912 | bytes 2678792 | tf_op jit(solution)/shard_map/pallas_call | solution.py:30
  45.0 11.5 %all_to_all.10 = f32[32,4,128]{2,1,0:T(4,128)S(1)} all-to-all(f32[32,4,128]{2,1,0:T(4,128)S(1)} %bitcast.11), channel_id=1, replica_groups=mesh['section'=4,'owner'=8] {'section','owner'}, dimensions={0} | all-to-all | bytes 131072 | tf_op jit(solution)/shard_map/all_to_all | solution.py:406
  56.5 0.6 %reduce_sum.9 = f32[4,128]{1,0:T(4,128)} reduce(f32[32,4,128]{2,1,0:T(4,128)S(1)} %all_to_all.10, f32[]{:T(128)} %constant.26.clone.1), dimensions={0}, to_apply=%region_0.0 | reduce | flops 15872 | bytes 67588 | tf_op jit(solution)/shard_map/reduce_sum | solution.py:407
  (21 shorter events, 0.0 us)
Async XLA Ops:
  0.0 14.3 %copy-start.4 = (s32[4096]{0:T(1024)S(1)}, s32[4096]{0:T(1024)}, u32[]{:S(2)}) copy-start(s32[4096]{0:T(1024)} %param.14) | copy-start | bytes 49156
  2.4 6.6 %collective-permute-start.2 = (bf16[192,128]{1,0:T(8,128)(2,1)}, bf16[192,128]{1,0:T(8,128)(2,1)S(1)}, u32[]{:S(2)}, u32[]{:S(2)}) collective-permute-start(bf16[192,128]{1,0:T(8,128)(2,1)} %get-tuple-element.16.refs_0_), channel_id=1, source_target_pairs={{24,0},{16,8},{8,16},{0,24},{25,1},{17,9},{9,17},{1,25},{26,2},{18... | collective-permute-start | bytes 147464 | tf_op jit(solution)/shard_map/ppermute | solution.py:343
  6.3 4.3 %collective-permute-start.1 = (bf16[192,128]{1,0:T(8,128)(2,1)}, bf16[192,128]{1,0:T(8,128)(2,1)S(1)}, u32[]{:S(2)}, u32[]{:S(2)}) collective-permute-start(bf16[192,128]{1,0:T(8,128)(2,1)} %get-tuple-element.16.refs_0_), channel_id=1, source_target_pairs={{16,0},{24,8},{0,16},{8,24},{17,1},{25,9},{1,17},{9,25},{18,2},{26... | collective-permute-start | bytes 147464 | tf_op jit(solution)/shard_map/ppermute | solution.py:343
  6.8 7.4 %collective-permute-start = (bf16[192,128]{1,0:T(8,128)(2,1)}, bf16[192,128]{1,0:T(8,128)(2,1)S(1)}, u32[]{:S(2)}, u32[]{:S(2)}) collective-permute-start(bf16[192,128]{1,0:T(8,128)(2,1)} %get-tuple-element.16.refs_0_), channel_id=1, source_target_pairs={{8,0},{0,8},{24,16},{16,24},{9,1},{1,9},{25,17},{17,25},{10,2},{2,... | collective-permute-start | bytes 147464 | tf_op jit(solution)/shard_map/ppermute | solution.py:343
  7.0 25.6 %collective-permute-start.5 = (bf16[528,128]{1,0:T(8,128)(2,1)}, bf16[528,128]{1,0:T(8,128)(2,1)S(1)}, u32[]{:S(2)}, u32[]{:S(2)}) collective-permute-start(bf16[528,128]{1,0:T(8,128)(2,1)} %get-tuple-element.21), channel_id=1, source_target_pairs={{0,2},{1,3},{2,0},{3,1},{4,6},{5,7},{6,4},{7,5},{8,10},{9,11},{10,... | collective-permute-start | bytes 405512 | tf_op jit(solution)/shard_map/ppermute | solution.py:337
  9.0 23.6 %collective-permute-start.6 = (bf16[528,128]{1,0:T(8,128)(2,1)}, bf16[528,128]{1,0:T(8,128)(2,1)S(1)}, u32[]{:S(2)}, u32[]{:S(2)}) collective-permute-start(bf16[528,128]{1,0:T(8,128)(2,1)} %get-tuple-element.22), channel_id=1, source_target_pairs={{0,3},{1,2},{2,1},{3,0},{4,7},{5,6},{6,5},{7,4},{8,11},{9,10},{10,... | collective-permute-start | bytes 405512 | tf_op jit(solution)/shard_map/ppermute | solution.py:337
  9.0 17.7 %collective-permute-start.7 = (bf16[528,128]{1,0:T(8,128)(2,1)}, bf16[528,128]{1,0:T(8,128)(2,1)S(1)}, u32[]{:S(2)}, u32[]{:S(2)}) collective-permute-start(bf16[528,128]{1,0:T(8,128)(2,1)} %get-tuple-element.24), channel_id=1, source_target_pairs={{0,1},{1,0},{2,3},{3,2},{4,5},{5,4},{6,7},{7,6},{8,9},{9,8},{10,11... | collective-permute-start | bytes 405512 | tf_op jit(solution)/shard_map/ppermute | solution.py:337
  10.6 19.0 %collective-permute-start.8 = (bf16[528,128]{1,0:T(8,128)(2,1)}, bf16[528,128]{1,0:T(8,128)(2,1)S(1)}, u32[]{:S(2)}, u32[]{:S(2)}) collective-permute-start(bf16[528,128]{1,0:T(8,128)(2,1)} %get-tuple-element.25), channel_id=1, source_target_pairs={{0,6},{1,7},{2,4},{3,5},{4,2},{5,3},{6,0},{7,1},{8,14},{9,15},{10,... | collective-permute-start | bytes 405512 | tf_op jit(solution)/shard_map/ppermute | solution.py:337
  14.2 15.4 %collective-permute-start.9 = (bf16[528,128]{1,0:T(8,128)(2,1)}, bf16[528,128]{1,0:T(8,128)(2,1)S(1)}, u32[]{:S(2)}, u32[]{:S(2)}) collective-permute-start(bf16[528,128]{1,0:T(8,128)(2,1)} %get-tuple-element.26), channel_id=1, source_target_pairs={{0,7},{1,6},{2,5},{3,4},{4,3},{5,2},{6,1},{7,0},{8,15},{9,14},{10,... | collective-permute-start | bytes 405512 | tf_op jit(solution)/shard_map/ppermute | solution.py:337
  14.3 1.2 %copy-start.3 = (bf16[4096,128]{1,0:T(8,128)(2,1)S(1)}, bf16[4096,128]{1,0:T(8,128)(2,1)}, u32[]{:S(2)}) copy-start(bf16[4096,128]{1,0:T(8,128)(2,1)} %values_ref.1) | copy-start | bytes 3145732
  15.5 14.2 %copy-start.5 = (bf16[528,128]{1,0:T(8,128)(2,1)S(1)}, bf16[528,128]{1,0:T(8,128)(2,1)}, u32[]{:S(2)}) copy-start(bf16[528,128]{1,0:T(8,128)(2,1)} %get-tuple-element.20) | copy-start | bytes 405508
  19.7 0.8 %copy-start.1 = (bf16[192,128]{1,0:T(8,128)(2,1)S(1)}, bf16[192,128]{1,0:T(8,128)(2,1)}, u32[]{:S(2)}) copy-start(bf16[192,128]{1,0:T(8,128)(2,1)} %get-tuple-element.16.refs_0_) | copy-start | bytes 147460
  19.8 0.8 %copy-start.2 = (s32[2,8,1]{1,2,0:T(1,128)S(1)}, s32[2,8,1]{1,2,0:T(1,128)}, u32[]{:S(2)}) copy-start(s32[2,8,1]{1,2,0:T(1,128)} %param.11) | copy-start | bytes 196
  19.8 6.9 %copy-start.6 = (bf16[528,128]{1,0:T(8,128)(2,1)S(1)}, bf16[528,128]{1,0:T(8,128)(2,1)}, u32[]{:S(2)}) copy-start(bf16[528,128]{1,0:T(8,128)(2,1)} %get-tuple-element.19) | copy-start | bytes 405508
  20.5 9.1 %copy-start = (bf16[528,128]{1,0:T(8,128)(2,1)S(1)}, bf16[528,128]{1,0:T(8,128)(2,1)}, u32[]{:S(2)}) copy-start(bf16[528,128]{1,0:T(8,128)(2,1)} %get-tuple-element.23.refs_0_.refs_2_) | copy-start | bytes 405508
  21.8 10.7 %all-to-all-start = ((f32[8,8,128]{2,1,0:T(8,128)}), f32[8,8,128]{2,1,0:T(8,128)S(1)}, u32[]{:S(2)}, u32[]{:S(2)}) async-start(f32[8,8,128]{2,1,0:T(8,128)} %get-tuple-element.17), calls=%async_computation | async-start | bytes 65536 | tf_op jit(solution)/shard_map/all_to_all | solution.py:358
  26.7 14.0 %collective-permute-start.3 = (bf16[528,128]{1,0:T(8,128)(2,1)S(1)}, bf16[528,128]{1,0:T(8,128)(2,1)S(1)}, u32[]{:S(2)}, u32[]{:S(2)}) collective-permute-start(bf16[528,128]{1,0:T(8,128)(2,1)S(1)} %copy-done.6), channel_id=1, source_target_pairs={{0,4},{1,5},{2,6},{3,7},{4,0},{5,1},{6,2},{7,3},{8,12},{9,13},{10,... | collective-permute-start | bytes 405512 | tf_op jit(solution)/shard_map/ppermute | solution.py:337
  29.7 12.8 %collective-permute-start.4 = (bf16[528,128]{1,0:T(8,128)(2,1)S(1)}, bf16[528,128]{1,0:T(8,128)(2,1)S(1)}, u32[]{:S(2)}, u32[]{:S(2)}) collective-permute-start(bf16[528,128]{1,0:T(8,128)(2,1)S(1)} %copy-done.5), channel_id=1, source_target_pairs={{0,5},{1,4},{2,7},{3,6},{4,1},{5,0},{6,3},{7,2},{8,13},{9,12},{10,... | collective-permute-start | bytes 405512 | tf_op jit(solution)/shard_map/ppermute | solution.py:337

commit v3 on v2

--- a/solution.py
+++ b/solution.py
@@ -183,14 +183,6 @@
     return values
 
 
-def join_rows(values, weights, rows, place_of, table_ref, found_ref):
-    count = values.shape[0] // rows
-    for block in range(count):
-        for row in range(rows):
-            found_ref[block * rows + row : block * rows + row + 1, :] = table_ref[pl.ds(place_of(block, row), 1), :]
-    return (chain(values, weights).astype(F32) * found_ref[...]).astype(BF16)
-
-
 def start_keys(parts, slots, span, keys_ref, places_ref, sem):
     for k, part in enumerate(parts):
         meta = part[span:, :].astype(F32)
@@ -200,16 +192,16 @@
     return copy
 
 
-def join_parts(parts, first, slots, span, weights, table_ref, found_ref, places_ref):
-    values = jnp.concatenate([part[:span, :] for part in parts], axis=0)
-    return join_rows(
-        values,
-        weights,
-        span // slots,
-        lambda block, row: places_ref[first + block // slots, block % slots, row],
-        table_ref,
-        found_ref,
-    )
+def join_parts(parts, first, slots, span, weights, table_ref, found_ref, places_ref, copy=None):
+    rows = span // slots
+    if copy is not None:
+        copy.wait()
+    values = chain(jnp.concatenate([part[:span, :] for part in parts], axis=0), weights)
+    for block in range(len(parts) * slots):
+        for row in range(rows):
+            place = places_ref[first + block // slots, block % slots, row]
+            found_ref[block * rows + row : block * rows + row + 1, :] = table_ref[pl.ds(place, 1), :]
+    return (values.astype(F32) * found_ref[...]).astype(BF16)
 
 
 def sums_of(parts, kepts, joined, slots, span, groups):
@@ -229,28 +221,26 @@
     group = found_ref.shape[0] // span
     copy = start_keys(parts, slots, span, keys_ref, places_ref, sem)
     weights = [weights_ref[j] for j in range(weights_ref.shape[0])]
-    copy.wait()
     for at in range(0, len(parts), group):
-        joined = join_parts(parts[at : at + group], at, slots, span, weights, table_ref, found_ref, places_ref)
+        first = None if at else copy
+        joined = join_parts(parts[at : at + group], at, slots, span, weights, table_ref, found_ref, places_ref, first)
         out_ref[at : at + group] = joined.reshape(group, span, joined.shape[1])
 
 
-def join_sum(slots, span, new, old, carried, scalar_ref, kept_ref, weights_ref, table_ref, *refs):
+def join_sum(slots, span, new, old, scalar_ref, kept_ref, weights_ref, table_ref, *refs):
     news, olds, refs = refs[: len(new)], refs[len(new) : len(new) + len(old)], refs[len(new) + len(old) :]
-    before, (out_ref, keys_ref, found_ref, places_ref, sem) = refs[:-5], refs[-5:]
+    joined_ref, out_ref, keys_ref, found_ref, places_ref, sem = refs
     groups = out_ref.shape[0]
     group = found_ref.shape[0] // span
     me = scalar_ref[weights_ref.shape[0]]
     copy = start_keys(news, slots, span, keys_ref, places_ref, sem)
     weights = [weights_ref[j] for j in range(weights_ref.shape[0])]
-    total = before[-1][...] if carried else jnp.zeros(out_ref.shape, F32)
-    if old:
-        joined = before[0][...].reshape(len(old) * span, out_ref.shape[1])
-        total += sums_of(olds, [kept_ref[me ^ k] for k in old], joined, slots, span, groups)
-    copy.wait()
+    joined = joined_ref[...].reshape(len(old) * span, out_ref.shape[1])
+    total = sums_of(olds, [kept_ref[me ^ k] for k in old], joined, slots, span, groups)
     for at in range(0, len(new), group):
         these = news[at : at + group]
-        joined = join_parts(these, at, slots, span, weights, table_ref, found_ref, places_ref)
+        first = None if at else copy
+        joined = join_parts(these, at, slots, span, weights, table_ref, found_ref, places_ref, first)
         total += sums_of(these, [kept_ref[me ^ k] for k in new[at : at + group]], joined, slots, span, groups)
     out_ref[...] = total
 
@@ -331,6 +321,7 @@
         ],
         scalars=(0,),
         away=True,
+        flops=40 * blocks.size * columns,
     )
     if few:
         for k in far_first(owners):
@@ -369,30 +360,22 @@
     sums_shape = ((groups_all, columns), F32)
     if few:
         order = far_first(owners)
-        near = [0, order[-1]]
-        soon, middle, final = near + order[: owners // 4], order[owners // 2 : -1], order[owners // 4 : owners // 2]
+        soon = [0, order[-1]] + order[: owners // 4]
+        rest = order[owners // 2 : -1] + order[owners // 4 : owners // 2]
         joined = run(
             functools.partial(join_only, slots),
             [weights, table] + [packed[k] for k in soon],
             ((len(soon), span, columns), BF16),
-            scratch(len(soon), 2),
+            scratch(len(soon), 4),
             flops=len(soon) * work,
         )
         sums = run(
-            functools.partial(join_sum, slots, span, middle, soon, False),
-            [scalars, kept, weights, table] + [packed[k] for k in middle + soon] + [joined],
+            functools.partial(join_sum, slots, span, rest, soon),
+            [scalars, kept, weights, table] + [packed[k] for k in rest + soon] + [joined],
             sums_shape,
-            scratch(len(middle), 2),
+            scratch(len(rest), 4),
             scalars=(0,),
-            flops=len(middle) * work,
-        )
-        sums = run(
-            functools.partial(join_sum, slots, span, final, [], True),
-            [scalars, kept, weights, table] + [packed[k] for k in final] + [sums],
-            sums_shape,
-            scratch(len(final), 2),
-            scalars=(0,),
-            flops=len(final) * work,
+            flops=len(rest) * work,
         )
     else:
         sums = run(

time: 57.4 us -> 54 us (0.941)
  starting transfers between devices: 18.2 us -> 16.5 us
  Pallas kernels: 15.8 us -> 14.4 us
  local copies, waits for them, and re-layouts: 1.98 us -> 0.77 us
  blocking collectives: 11.5 us -> 12.5 us
    ppermute x7, waiting for transfers between devices: 7.2 us -> 0.02 us  [local(): lax.ppermute(packed[k], 'owner', [(i, i ^ k) for i in range(owners)])]
    all_to_all x1, waiting for transfers between devices: 0.16 us -> 4.99 us  [local(): lax.all_to_all(kept, 'owner', split_axis=0, concat_axis=0, tiled=True)]
    ppermute x3, waiting for transfers between devices: 1.52 us -> 3.76 us  [local(): lax.ppermute(shared, 'section', [(partner(i, k), i) for i in range(sectio...]
    pallas_call x6 -> x5, Pallas kernels: 15.8 us -> 14.4 us  [run(): pl.pallas_call(kernel, out_shape=shapes if several else shapes[0], in_spe...]
    unnamed x14 -> x10, local copies, waits for them, and re-layouts: 1.89 us -> 0.68 us
    ppermute x3, starting transfers between devices: 4.63 us -> 3.49 us  [local(): lax.ppermute(shared, 'section', [(partner(i, k), i) for i in range(sectio...]
    all_to_all x1, blocking collectives: 11.5 us -> 12.5 us  [local(): lax.all_to_all(parts, ('section', 'owner'), split_axis=0, concat_axis=0,...]
  transfers between devices with their start and end apart: 11 -> 11, of which waited for: 4 -> 4; matrix products, arithmetic and copies ran while one was open for 0% -> 0% of each run, Pallas kernels for 19% -> 15%
where the time goes in v3:
time: 54 us; the launch traced here: 53.7 us
  starting transfers between devices  16.5 us (31%)
  Pallas kernels  14.4 us (27%)
  blocking collectives  12.5 us (23%)
  waiting for transfers between devices  8.77 us (16%)
  local copies, waits for them, and re-layouts  0.77 us (1%)
  other arithmetic  0.62 us (1%)
    pallas_call x5, Pallas kernels, run(): pl.pallas_call(kernel, out_shape=shapes if several else shapes[0], in_spe...  14.4 us
    all_to_all x1, blocking collectives, local(): lax.all_to_all(parts, ('section', 'owner'), split_axis=0, concat_axis=0,...  12.5 us
    ppermute x7, starting transfers between devices, local(): lax.ppermute(packed[k], 'owner', [(i, i ^ k) for i in range(owners)])  8.62 us
    all_to_all x1, waiting for transfers between devices, local(): lax.all_to_all(kept, 'owner', split_axis=0, concat_axis=0, tiled=True)  4.99 us
    all_to_all x1, starting transfers between devices, local(): lax.all_to_all(kept, 'owner', split_axis=0, concat_axis=0, tiled=True)  4.36 us
    ppermute x3, waiting for transfers between devices, local(): lax.ppermute(shared, 'section', [(partner(i, k), i) for i in range(sectio...  3.76 us
    ppermute x3, starting transfers between devices, local(): lax.ppermute(shared, 'section', [(partner(i, k), i) for i in range(sectio...  3.49 us
  transfers between devices with their start and end apart: 11, of which 4 were waited for; matrix products, arithmetic and copies ran while one was open for 0% of the time, Pallas kernels for 15%

profile of v3, /device:TPU:0, one launch (start us, length us, event | category | flops | bytes accessed | tf_op | source)
XLA Modules:
  0.0 53.7 jit_solution(5983718222404669693)
XLA Ops:
  0.0 2.4 %shard_map.82 = (bf16[192,128]{1,0:T(8,128)(2,1)}, bf16[528,128]{1,0:T(8,128)(2,1)}, bf16[528,128]{1,0:T(8,128)(2,1)}, bf16[528,128]{1,0:T(8,128)(2,1)}, bf16[52...) custom-call(s32[1]{0:T(128)} %bitcast.3.me_ref, ...), custom_call_target="tpu_custom_call" | custom-call | flops 1342177280 | bytes 7852272 | tf_op jit(solution)/shard_map/pallas_call | solution.py:30
  2.4 0.0 copy-start.3
  2.4 0.6 %collective-permute-start.7 = (bf16[528,128]{1,0:T(8,128)(2,1)}, bf16[528,128]{1,0:T(8,128)(2,1)S(1)}, u32[]{:S(2)}, u32[]{:S(2)}) collective-permute-start(bf16[528,128]{1,0:T(8,128)(2,1)} %get-tuple-element.24), channel_id=1, source_target_pairs={{0,1},{1,0},{2,3},{3,2},{4,5},{5,4},{6,7},{7,6},{8,9},{9,8},{10,11... | collective-permute-start | bytes 405512 | tf_op jit(solution)/shard_map/ppermute | solution.py:328
  3.0 4.7 %collective-permute-start.8 = (bf16[528,128]{1,0:T(8,128)(2,1)}, bf16[528,128]{1,0:T(8,128)(2,1)S(1)}, u32[]{:S(2)}, u32[]{:S(2)}) collective-permute-start(bf16[528,128]{1,0:T(8,128)(2,1)} %get-tuple-element.25), channel_id=1, source_target_pairs={{0,6},{1,7},{2,4},{3,5},{4,2},{5,3},{6,0},{7,1},{8,14},{9,15},{10,... | collective-permute-start | bytes 405512 | tf_op jit(solution)/shard_map/ppermute | solution.py:328
  7.6 2.4 %collective-permute-start.2 = (bf16[192,128]{1,0:T(8,128)(2,1)}, bf16[192,128]{1,0:T(8,128)(2,1)S(1)}, u32[]{:S(2)}, u32[]{:S(2)}) collective-permute-start(bf16[192,128]{1,0:T(8,128)(2,1)} %get-tuple-element.16.refs_0_), channel_id=1, source_target_pairs={{24,0},{16,8},{8,16},{0,24},{25,1},{17,9},{9,17},{1,25},{26,2},{18... | collective-permute-start | bytes 147464 | tf_op jit(solution)/shard_map/ppermute | solution.py:334
  10.1 0.5 collective-permute-start.1
  10.6 0.5 collective-permute-start
  11.1 1.7 %collective-permute-done.2.refs_3_ = bf16[192,128]{1,0:T(8,128)(2,1)S(1)} collective-permute-done((bf16[192,128]{1,0:T(8,128)(2,1)}, bf16[192,128]{1,0:T(8,128)(2,1)S(1)}, u32[]{:S(2)}, u32[]{:S(2)}) %collective-permute-start.2) | collective-permute-done | bytes 49184 | tf_op jit(solution)/shard_map/ppermute | solution.py:334
  12.9 1.5 %collective-permute-done.1.refs_2_ = bf16[192,128]{1,0:T(8,128)(2,1)S(1)} collective-permute-done((bf16[192,128]{1,0:T(8,128)(2,1)}, bf16[192,128]{1,0:T(8,128)(2,1)S(1)}, u32[]{:S(2)}, u32[]{:S(2)}) %collective-permute-start.1) | collective-permute-done | bytes 49184 | tf_op jit(solution)/shard_map/ppermute | solution.py:334
  14.4 0.0 collective-permute-start.4
  14.4 0.5 collective-permute-done.refs_1_
  14.9 2.3 %collective-permute-start.6 = (bf16[528,128]{1,0:T(8,128)(2,1)}, bf16[528,128]{1,0:T(8,128)(2,1)S(1)}, u32[]{:S(2)}, u32[]{:S(2)}) collective-permute-start(bf16[528,128]{1,0:T(8,128)(2,1)} %get-tuple-element.22), channel_id=1, source_target_pairs={{0,5},{1,4},{2,7},{3,6},{4,1},{5,0},{6,3},{7,2},{8,13},{9,12},{10,... | collective-permute-start | bytes 405512 | tf_op jit(solution)/shard_map/ppermute | solution.py:328
  17.3 1.0 %collective-permute-start.9 = (bf16[528,128]{1,0:T(8,128)(2,1)}, bf16[528,128]{1,0:T(8,128)(2,1)S(1)}, u32[]{:S(2)}, u32[]{:S(2)}) collective-permute-start(bf16[528,128]{1,0:T(8,128)(2,1)} %get-tuple-element.26), channel_id=1, source_target_pairs={{0,7},{1,6},{2,5},{3,4},{4,3},{5,2},{6,1},{7,0},{8,15},{9,14},{10,... | collective-permute-start | bytes 405512 | tf_op jit(solution)/shard_map/ppermute | solution.py:328
  18.3 4.2 %shard_map.84.table_ref = f32[2048,128]{1,0:T(8,128)S(1)} custom-call(s32[32,128]{1,0:T(8,128)S(1)} %bitcast.14, bf16[4096,128]{1,0:T(8,128)(2,1)S(1)} %copy-done.2), custom_call_target="tpu_custom_call" | custom-call | flops 2147483648 | bytes 10502144 | tf_op jit(solution)/shard_map/pallas_call | solution.py:30
  22.6 0.0 copy-start.1
  22.6 0.1 stack.23.scalar_ref
  22.7 0.7 %copy-done = bf16[192,128]{1,0:T(8,128)(2,1)S(1)} copy-done((bf16[192,128]{1,0:T(8,128)(2,1)S(1)}, bf16[192,128]{1,0:T(8,128)(2,1)}, u32[]{:S(2)}) %copy-start) | copy-done | bytes 49176
  23.3 1.3 %shard_map.83 = (bf16[4,128,128]{2,1,0:T(8,128)(2,1)S(1)}, f32[8,8,128]{2,1,0:T(8,128)}) custom-call(s32[6]{0:T(128)S(1)} %stack.23.scalar_ref, bf16[192,128]{1,0:T(8,128)(2,1)S(1)} %copy-done, bf16[192,128]{1,0:T(8,128)(2,1)S(1)} %collective-permute-done.refs_1_, bf16[192,128]{1,0:T(8,128)(2,1)S(1)} %collective-permute-done.1.refs_2_, ...), custom_call_target="tpu_custom_call" | custom-call | tf_op jit(solution)/shard_map/pallas_call | solution.py:30
  24.7 4.4 %all-to-all-start = ((f32[8,8,128]{2,1,0:T(8,128)}), f32[8,8,128]{2,1,0:T(8,128)S(1)}, u32[]{:S(2)}, u32[]{:S(2)}) async-start(f32[8,8,128]{2,1,0:T(8,128)} %get-tuple-element.17), calls=%async_computation | async-start | bytes 65536 | tf_op jit(solution)/shard_map/all_to_all | solution.py:349
  29.0 2.8 %shard_map.85.refs_8_ = bf16[4,512,128]{2,1,0:T(8,128)(2,1)S(1)} custom-call(bf16[4,128,128]{2,1,0:T(8,128)(2,1)S(1)} %get-tuple-element.18.weights_ref, f32[2048,128]{1,0:T(8,128)S(1)} %shard_map.84.table_ref, bf16[528,128]{1,0:T(8,128)(2,1)S(1)} %copy-done.4, bf16[528,128]{1,0:T(8,128)(2,1)S(1)} %collective-permute-done.7.refs_1_.refs_5_, ...), custom_call_target="tpu_custom_call" | custom-call | flops 1073741824 | bytes 4374536 | tf_op jit(solution)/shard_map/pallas_call | solution.py:30
  31.8 5.0 %all-to-all-done.kept_ref = f32[8,8,128]{2,1,0:T(8,128)S(1)} async-done(((f32[8,8,128]{2,1,0:T(8,128)}), f32[8,8,128]{2,1,0:T(8,128)S(1)}, u32[]{:S(2)}, u32[]{:S(2)}) %all-to-all-start) | async-done | bytes 32800 | tf_op jit(solution)/shard_map/all_to_all | solution.py:349
  36.8 3.7 %shard_map.86 = f32[128,128]{1,0:T(8,128)S(1)} custom-call(s32[6]{0:T(128)S(1)} %stack.23.scalar_ref, f32[8,8,128]{2,1,0:T(8,128)S(1)} %all-to-all-done.kept_ref, bf16[4,128,128]{2,1,0:T(8,128)(2,1)S(1)} %get-tuple-element.18.weights_ref, f32[2048,128]{1,0:T(8,128)S(1)} %shard_map.84.table_ref, bf16[528,128]{1,0:T(8,128)(2,1)S(1)} %collective-permute-done.3.refs_0_, ...), custom_call_target="tpu_custom_call" | custom-call | flops 1073741824 | bytes 5013512 | tf_op jit(solution)/shard_map/pallas_call | solution.py:30
  40.6 12.5 %all_to_all.10 = f32[32,4,128]{2,1,0:T(4,128)S(1)} all-to-all(f32[32,4,128]{2,1,0:T(4,128)S(1)} %bitcast.11), channel_id=1, replica_groups=mesh['section'=4,'owner'=8] {'section','owner'}, dimensions={0} | all-to-all | bytes 131072 | tf_op jit(solution)/shard_map/all_to_all | solution.py:389
  53.1 0.6 %reduce_sum.9 = f32[4,128]{1,0:T(4,128)} reduce(f32[32,4,128]{2,1,0:T(4,128)S(1)} %all_to_all.10, f32[]{:T(128)} %constant.26.clone.1), dimensions={0}, to_apply=%region_0.0 | reduce | flops 15872 | bytes 67588 | tf_op jit(solution)/shard_map/reduce_sum | solution.py:390
  (16 shorter events, 0.0 us)
Async XLA Ops:
  0.0 18.3 %copy-start.2 = (bf16[4096,128]{1,0:T(8,128)(2,1)S(1)}, bf16[4096,128]{1,0:T(8,128)(2,1)}, u32[]{:S(2)}) copy-start(bf16[4096,128]{1,0:T(8,128)(2,1)} %values_ref.1) | copy-start | bytes 3145732
  2.4 15.9 %copy-start.3 = (s32[4096]{0:T(1024)S(1)}, s32[4096]{0:T(1024)}, u32[]{:S(2)}) copy-start(s32[4096]{0:T(1024)} %param.14) | copy-start | bytes 49156
  2.4 12.5 %collective-permute-start.7 = (bf16[528,128]{1,0:T(8,128)(2,1)}, bf16[528,128]{1,0:T(8,128)(2,1)S(1)}, u32[]{:S(2)}, u32[]{:S(2)}) collective-permute-start(bf16[528,128]{1,0:T(8,128)(2,1)} %get-tuple-element.24), channel_id=1, source_target_pairs={{0,1},{1,0},{2,3},{3,2},{4,5},{5,4},{6,7},{7,6},{8,9},{9,8},{10,11... | collective-permute-start | bytes 405512 | tf_op jit(solution)/shard_map/ppermute | solution.py:328
  3.0 14.3 %collective-permute-start.8 = (bf16[528,128]{1,0:T(8,128)(2,1)}, bf16[528,128]{1,0:T(8,128)(2,1)S(1)}, u32[]{:S(2)}, u32[]{:S(2)}) collective-permute-start(bf16[528,128]{1,0:T(8,128)(2,1)} %get-tuple-element.25), channel_id=1, source_target_pairs={{0,6},{1,7},{2,4},{3,5},{4,2},{5,3},{6,0},{7,1},{8,14},{9,15},{10,... | collective-permute-start | bytes 405512 | tf_op jit(solution)/shard_map/ppermute | solution.py:328
  7.6 5.2 %collective-permute-start.2 = (bf16[192,128]{1,0:T(8,128)(2,1)}, bf16[192,128]{1,0:T(8,128)(2,1)S(1)}, u32[]{:S(2)}, u32[]{:S(2)}) collective-permute-start(bf16[192,128]{1,0:T(8,128)(2,1)} %get-tuple-element.16.refs_0_), channel_id=1, source_target_pairs={{24,0},{16,8},{8,16},{0,24},{25,1},{17,9},{9,17},{1,25},{26,2},{18... | collective-permute-start | bytes 147464 | tf_op jit(solution)/shard_map/ppermute | solution.py:334
  10.1 4.3 %collective-permute-start.1 = (bf16[192,128]{1,0:T(8,128)(2,1)}, bf16[192,128]{1,0:T(8,128)(2,1)S(1)}, u32[]{:S(2)}, u32[]{:S(2)}) collective-permute-start(bf16[192,128]{1,0:T(8,128)(2,1)} %get-tuple-element.16.refs_0_), channel_id=1, source_target_pairs={{16,0},{24,8},{0,16},{8,24},{17,1},{25,9},{1,17},{9,25},{18,2},{26... | collective-permute-start | bytes 147464 | tf_op jit(solution)/shard_map/ppermute | solution.py:334
  10.6 4.3 %collective-permute-start = (bf16[192,128]{1,0:T(8,128)(2,1)}, bf16[192,128]{1,0:T(8,128)(2,1)S(1)}, u32[]{:S(2)}, u32[]{:S(2)}) collective-permute-start(bf16[192,128]{1,0:T(8,128)(2,1)} %get-tuple-element.16.refs_0_), channel_id=1, source_target_pairs={{8,0},{0,8},{24,16},{16,24},{9,1},{1,9},{25,17},{17,25},{10,2},{2,... | collective-permute-start | bytes 147464 | tf_op jit(solution)/shard_map/ppermute | solution.py:334
  12.9 24.0 %collective-permute-start.3 = (bf16[528,128]{1,0:T(8,128)(2,1)}, bf16[528,128]{1,0:T(8,128)(2,1)S(1)}, u32[]{:S(2)}, u32[]{:S(2)}) collective-permute-start(bf16[528,128]{1,0:T(8,128)(2,1)} %get-tuple-element.19), channel_id=1, source_target_pairs={{0,2},{1,3},{2,0},{3,1},{4,6},{5,7},{6,4},{7,5},{8,10},{9,11},{10,... | collective-permute-start | bytes 405512 | tf_op jit(solution)/shard_map/ppermute | solution.py:328
  14.4 22.4 %collective-permute-start.4 = (bf16[528,128]{1,0:T(8,128)(2,1)}, bf16[528,128]{1,0:T(8,128)(2,1)S(1)}, u32[]{:S(2)}, u32[]{:S(2)}) collective-permute-start(bf16[528,128]{1,0:T(8,128)(2,1)} %get-tuple-element.20), channel_id=1, source_target_pairs={{0,3},{1,2},{2,1},{3,0},{4,7},{5,6},{6,5},{7,4},{8,11},{9,10},{10,... | collective-permute-start | bytes 405512 | tf_op jit(solution)/shard_map/ppermute | solution.py:328
  14.9 21.9 %collective-permute-start.5 = (bf16[528,128]{1,0:T(8,128)(2,1)}, bf16[528,128]{1,0:T(8,128)(2,1)S(1)}, u32[]{:S(2)}, u32[]{:S(2)}) collective-permute-start(bf16[528,128]{1,0:T(8,128)(2,1)} %get-tuple-element.21), channel_id=1, source_target_pairs={{0,4},{1,5},{2,6},{3,7},{4,0},{5,1},{6,2},{7,3},{8,12},{9,13},{10,... | collective-permute-start | bytes 405512 | tf_op jit(solution)/shard_map/ppermute | solution.py:328
  14.9 21.9 %collective-permute-start.6 = (bf16[528,128]{1,0:T(8,128)(2,1)}, bf16[528,128]{1,0:T(8,128)(2,1)S(1)}, u32[]{:S(2)}, u32[]{:S(2)}) collective-permute-start(bf16[528,128]{1,0:T(8,128)(2,1)} %get-tuple-element.22), channel_id=1, source_target_pairs={{0,5},{1,4},{2,7},{3,6},{4,1},{5,0},{6,3},{7,2},{8,13},{9,12},{10,... | collective-permute-start | bytes 405512 | tf_op jit(solution)/shard_map/ppermute | solution.py:328
  17.3 11.8 %collective-permute-start.9 = (bf16[528,128]{1,0:T(8,128)(2,1)}, bf16[528,128]{1,0:T(8,128)(2,1)S(1)}, u32[]{:S(2)}, u32[]{:S(2)}) collective-permute-start(bf16[528,128]{1,0:T(8,128)(2,1)} %get-tuple-element.26), channel_id=1, source_target_pairs={{0,7},{1,6},{2,5},{3,4},{4,3},{5,2},{6,1},{7,0},{8,15},{9,14},{10,... | collective-permute-start | bytes 405512 | tf_op jit(solution)/shard_map/ppermute | solution.py:328
  22.5 0.8 %copy-start = (bf16[192,128]{1,0:T(8,128)(2,1)S(1)}, bf16[192,128]{1,0:T(8,128)(2,1)}, u32[]{:S(2)}) copy-start(bf16[192,128]{1,0:T(8,128)(2,1)} %get-tuple-element.16.refs_0_) | copy-start | bytes 147460
  22.6 0.8 %copy-start.1 = (s32[2,8,1]{1,2,0:T(1,128)S(1)}, s32[2,8,1]{1,2,0:T(1,128)}, u32[]{:S(2)}) copy-start(s32[2,8,1]{1,2,0:T(1,128)} %param.11) | copy-start | bytes 196
  23.3 5.7 %copy-start.4 = (bf16[528,128]{1,0:T(8,128)(2,1)S(1)}, bf16[528,128]{1,0:T(8,128)(2,1)}, u32[]{:S(2)}) copy-start(bf16[528,128]{1,0:T(8,128)(2,1)} %get-tuple-element.23.refs_0_.refs_4_) | copy-start | bytes 405508
  24.7 12.2 %all-to-all-start = ((f32[8,8,128]{2,1,0:T(8,128)}), f32[8,8,128]{2,1,0:T(8,128)S(1)}, u32[]{:S(2)}, u32[]{:S(2)}) async-start(f32[8,8,128]{2,1,0:T(8,128)} %get-tuple-element.17), calls=%async_computation | async-start | bytes 65536 | tf_op jit(solution)/shard_map/all_to_all | solution.py:349
